TPU v7x, 128 devices: a whole 4x4x4 slice. The times are simulated.
128 devices in a mesh: dp: 16 (over y_hi, x, core), expert: 8 (over z, y_lo).
Axes of the slice: x: 4, y: 4 (y_hi: 2, y_lo: 2; y = y_hi * 2 + y_lo), z: 4, core: 2. Of those that a mesh axis runs over, the one named last changes fastest.
Arguments:
- tokens: bfloat16 [32, 2048, 4096], P('dp', 'expert'), may hold values from -6 to 6
- out_grad: bfloat16 [32, 2048, 4096], P('dp', 'expert'), may hold values from -6 to 6
- router: bfloat16 [4096, 8], replicated, may hold values from -4 to 4
- weight_in: bfloat16 [8, 4096, 512], P('expert', 'dp'), may hold values from -0.09375 to 0.09375
- weight_out: bfloat16 [8, 4096, 512], P('expert', 'dp'), may hold values from -0.25 to 0.25
Outputs:
- token_grad: bfloat16 [32, 2048, 4096], P(None, ('expert', 'dp'))
- grad_in: float32 [8, 4096, 512], P('expert', 'dp')
- grad_out: float32 [8, 4096, 512], P('expert', 'dp')
All inputs are finite; a program needn't handle non-finite values.
Results may differ from a plain program's by a relative error of at most 0.022.
Values may be sent and summed in bfloat16 or wider, within the bound.
No kernel may reach another device: no remote copies, remote signals or barrier semaphores. Data moves between devices by JAX's collectives and lax.ppermute only.
A program may use at most 128 MiB of HBM per device.

v0:
```python
import jax
import jax.numpy as jnp
from jax import lax
from jax.experimental import pallas as pl
from jax.experimental.pallas import tpu as pltpu
from jax.sharding import Mesh
from jax.sharding import PartitionSpec as P

BF = jnp.bfloat16
F32 = jnp.float32
D = 4096
HALF = 2048
HID = 512
SEQS = 32
EXPERTS = 8
POS = 16
ROWS = SEQS * POS
LANES = EXPERTS * POS
SHARD = 256
MIB = 1024 * 1024
ORDER = (2, 1, 3, 0)
VM = pl.BlockSpec(memory_space=pltpu.VMEM)
HBM = pl.BlockSpec(memory_space=pltpu.HBM)


def call(kernel, outs, n_in, flops, nbytes, vmem, scratch=(), specs=None, far=0):
    return pl.pallas_call(
        kernel,
        out_shape=outs,
        in_specs=[VM] * n_in + [HBM] * far,
        out_specs=specs or jax.tree.map(lambda _: VM, outs),
        scratch_shapes=scratch,
        compiler_params=pltpu.CompilerParams(vmem_limit_bytes=vmem * MIB),
        cost_estimate=pl.CostEstimate(flops=flops, bytes_accessed=nbytes, transcendentals=0),
    )


def shape(dims, dtype):
    return jax.ShapeDtypeStruct(dims, dtype)


def in_hbm(x):
    return pltpu.with_memory_space_constraint(x, pltpu.HBM)


def nt(a, b):
    return lax.dot_general(a, b, (((1,), (1,)), ((), ())), preferred_element_type=F32)


def tn(a, b):
    return lax.dot_general(a, b, (((0,), (0,)), ((), ())), preferred_element_type=F32)


def pack_kernel(t_ref, g_ref, wi_ref, wo_ref, router_ref, o_ref, w_ref, rxt_ref, sem):
    copies = []
    for i in range(16):
        src, seq, part = (t_ref, g_ref)[i // 8], i // 4 % 2, pl.ds(i % 4 * 4, 4)
        copies.append(pltpu.make_async_copy(src.at[seq, part], o_ref.at[part, i // 4], sem.at[i]))
    copies.append(pltpu.make_async_copy(wi_ref.at[0], w_ref.at[0], sem.at[16]))
    copies.append(pltpu.make_async_copy(wo_ref.at[0], w_ref.at[1], sem.at[17]))
    for copy in copies:
        copy.start()
    for e in range(EXPERTS):
        row = router_ref[e : e + 1, :].astype(F32)
        rxt_ref[e * POS : (e + 1) * POS, :] = jnp.broadcast_to(row, (POS, D)).astype(BF)
    for copy in copies:
        copy.wait()


def pack(tokens, out_grad, weight_in, weight_out, router):
    blocks = (2, 16, POS, D)
    arrays = (tokens.reshape(blocks), out_grad.reshape(blocks), weight_in, weight_out)
    return pl.pallas_call(
        pack_kernel,
        out_shape=(shape((16, 4, POS, D), BF), shape((2, SHARD, HID), BF), shape((LANES, D), BF)),
        in_specs=[HBM] * 4 + [VM],
        out_specs=(VM, VM, VM),
        scratch_shapes=[pltpu.SemaphoreType.DMA((18,))],
        cost_estimate=pl.CostEstimate(flops=8 * MIB, bytes_accessed=16 * MIB, transcendentals=0),
        compiler_params=pltpu.CompilerParams(vmem_limit_bytes=16 * MIB),
        name="pack",
    )(*[in_hbm(a) for a in arrays], router.T)


def own_position():
    row = lax.broadcasted_iota(jnp.int32, (POS, LANES), 0)
    lane = lax.broadcasted_iota(jnp.int32, (POS, LANES), 1)
    return (lane % POS == row)[None]


def mix_kernel(a_ref, rxt_ref, f_ref, probs_ref, mixing_ref, held, sem):
    logits = jnp.zeros((LANES, ROWS), F32)
    for j in range(4):
        cols = pl.ds(j * 1024, 1024)
        logits += nt(rxt_ref[:, cols], a_ref[:, 0:2, :, cols].reshape(ROWS, 1024))
    logits = logits.T.reshape(SEQS, POS, LANES)
    weights = jnp.exp(logits - jnp.max(logits, axis=0, keepdims=True))
    probs = weights / jnp.sum(weights, axis=0, keepdims=True)
    probs = jnp.where(own_position(), probs, 0.0).reshape(ROWS, LANES)
    probs_ref[...] = probs
    mixing_ref[...] = probs.astype(BF)
    mixing_t = probs.T.astype(BF)
    copies = []
    for j in range(8):
        cols = pl.ds(j * 512, 512)
        half, part = j // 4, pl.ds(j % 4 * 512, 512)
        for t in range(2):
            block = a_ref[:, 2 * t : 2 * t + 2, :, cols].reshape(ROWS, 512)
            mixed = jnp.dot(mixing_t, block, preferred_element_type=F32)
            held[half, :, t, :, part] = mixed.astype(BF).reshape(EXPERTS, POS, 512)
        place = (half, slice(None), slice(None), slice(None), part)
        copies.append(pltpu.make_async_copy(held.at[place], f_ref.at[place], sem.at[j]))
        copies[j].start()
    for copy in copies:
        copy.wait()


def shard_columns(k, j):
    owner = lax.rem(lax.axis_index("x") + 4 - k, 4) * 2 + lax.rem(lax.axis_index("c") + j, 2)
    return pl.ds(pl.multiple_of(owner * SHARD, SHARD), SHARD)


def partial_kernel(f_ref, *refs):
    shard_refs, (own_ref, send_ref, w_ref, sem) = refs[:8], refs[8:]
    copies = [pltpu.make_async_copy(ref, w_ref.at[i], sem.at[i]) for i, ref in enumerate(shard_refs)]
    for copy in copies:
        copy.start()
    sums = [jnp.zeros((256, HID), F32) for _ in range(2)]
    for i, copy in enumerate(copies):
        cols = shard_columns(i // 2, i % 2)
        copy.wait()
        for t in range(2):
            block = f_ref[:, t, :, cols].reshape(256, SHARD)
            sums[t] += jnp.dot(block, w_ref[i, t], preferred_element_type=F32)
    for t in range(2):
        own_ref[t] = sums[t]
        send_ref[t] = sums[t].astype(BF)


def expert_kernel(own_ref, other_ref, w_ref, b_ref, hidden_ref, held, sem):
    pre = own_ref[0] + other_ref[0].astype(F32)
    hidden_full = own_ref[1] + other_ref[1].astype(F32)
    sigma = jax.nn.sigmoid(pre)
    hidden = (pre * sigma).astype(BF)
    hidden_grad = (hidden_full * sigma * (1.0 + pre * (1.0 - sigma))).astype(BF)
    hidden_ref[0] = hidden_grad
    hidden_ref[1] = hidden
    copies = []
    for i in range(8):
        cols = shard_columns(i // 2, i % 2)
        held[:, 0, :, cols] = nt(hidden, w_ref[i, 1]).astype(BF).reshape(16, POS, SHARD)
        held[:, 1, :, cols] = nt(hidden_grad, w_ref[i, 0]).astype(BF).reshape(16, POS, SHARD)
        place = (slice(None), slice(None), slice(None), cols)
        copies.append(pltpu.make_async_copy(held.at[place], b_ref.at[place], sem.at[i]))
        copies[i].start()
    for copy in copies:
        copy.wait()


def grads_kernel(f_ref, hidden_ref, *out_refs):
    for n, k in enumerate(ORDER):
        for j in range(2):
            cols = shard_columns(4 - k, j)
            for t in range(2):
                block = f_ref[:, t, :, cols].reshape(256, SHARD)
                out_refs[2 * n + j][t] = tn(block, hidden_ref[t]).astype(BF)


def add_kernel(keep_ref, got_ref, o_ref):
    o_ref[...] = (keep_ref[...].astype(F32) + got_ref[...].astype(F32)).astype(o_ref.dtype)


def sum_kernel(own_ref, a_ref, b_ref, c_ref, in_ref, out_ref):
    for t, ref in enumerate((in_ref, out_ref)):
        ref[0] = own_ref[t] + a_ref[t].astype(F32) + b_ref[t].astype(F32) + c_ref[t].astype(F32)


def final_kernel(b_ref, probs_ref, mixing_ref, rows_ref, far_rxt_ref, o_ref, a_ref, rxt_ref, held, in_sem, sem):
    reads = []
    for j in range(8):
        cols = pl.ds(j * 512, 512)
        reads.append(pltpu.make_async_copy(rows_ref.at[..., cols], a_ref.at[..., cols], in_sem.at[j]))
    reads.append(pltpu.make_async_copy(far_rxt_ref, rxt_ref, in_sem.at[8]))
    for copy in reads:
        copy.start()
    weight_grad = jnp.zeros((LANES, ROWS), F32)
    for j in range(8):
        cols = pl.ds(j * 512, 512)
        reads[j].wait()
        half, part = pl.ds(j // 4 * EXPERTS, EXPERTS), pl.ds(j % 4 * 512, 512)
        for t in range(2):
            block = a_ref[:, 2 - 2 * t : 4 - 2 * t, :, cols].reshape(ROWS, 512)
            weight_grad += nt(b_ref[half, t, :, part].reshape(LANES, 512), block)
    probs = probs_ref[...].reshape(SEQS, POS, LANES)
    weight_grad = weight_grad.T.reshape(SEQS, POS, LANES)
    mean = jnp.sum(probs * weight_grad, axis=0, keepdims=True)
    logit_grad = (probs * (weight_grad - mean)).reshape(ROWS, LANES).astype(BF)
    both = jnp.concatenate([mixing_ref[...], logit_grad], axis=1)
    reads[8].wait()
    copies = []
    for j in range(8):
        cols = pl.ds(j * 512, 512)
        half, part = pl.ds(j // 4 * EXPERTS, EXPERTS), pl.ds(j % 4 * 512, 512)
        right = jnp.concatenate([b_ref[half, 1, :, part].reshape(LANES, 512), rxt_ref[:, cols]], axis=0)
        out = jnp.dot(both, right, preferred_element_type=F32)
        held[:, :, cols] = out.astype(BF).reshape(SEQS, POS, 512)
        copies.append(pltpu.make_async_copy(held.at[:, :, cols], o_ref.at[:, :, cols], sem.at[j]))
        copies[j].start()
    for copy in copies:
        copy.wait()


def shift(x, k):
    return lax.ppermute(x, "x", [(i, (i + k) % 4) for i in range(4)])


def swap(x, axis):
    return lax.ppermute(x, axis, [(0, 1), (1, 0)])


def on_device(tokens, out_grad, router, weight_in, weight_out):
    rows, shard, rxt = pack(tokens, out_grad, weight_in, weight_out, router)
    rows = lax.all_to_all(rows, ("yh", "x", "c"), 0, 0, tiled=True)
    mixed, probs, mixing = call(
        mix_kernel,
        (pltpu.HBM((2, EXPERTS, 2, POS, HALF), BF), shape((ROWS, LANES), F32), shape((ROWS, LANES), BF)),
        2, 3 * 10**9, 12 * MIB, 22, specs=(HBM, VM, VM),
        scratch=[pltpu.VMEM((2, EXPERTS, 2, POS, HALF), BF), pltpu.SemaphoreType.DMA((8,))],
    )(rows, rxt)

    experts = ("yh", "z", "yl")
    got = lax.all_to_all(mixed.reshape(16, 2, POS, HALF), experts, 0, 0, tiled=True)

    shard, _ = lax.optimization_barrier((shard, mixing))
    shards = [shard] + [shift(shard, k) for k in range(1, 4)]
    weights = []
    for w in shards:
        weights += [w, swap(w, "c")]

    own, send, weights = call(
        partial_kernel,
        (shape((2, 256, HID), F32), shape((2, 256, HID), BF), shape((8, 2, SHARD, HID), BF)),
        1, 10**9, 8 * MIB, 14, far=8,
        scratch=[pltpu.SemaphoreType.DMA((8,))],
    )(got, *[in_hbm(w) for w in weights])
    other = swap(send, "yh")
    back, hidden = call(
        expert_kernel,
        (pltpu.HBM((16, 2, POS, HALF), BF), shape((2, 256, HID), BF)),
        3, 10**9, 8 * MIB, 16, specs=(HBM, VM),
        scratch=[pltpu.VMEM((16, 2, POS, HALF), BF), pltpu.SemaphoreType.DMA((8,))],
    )(own, other, weights)
    back = lax.all_to_all(back, experts, 0, 0, tiled=True)

    piece = shape((2, SHARD, HID), BF)
    parts = call(grads_kernel, (piece,) * 8, 2, 10**9, 8 * MIB, 14)(got, hidden)
    sums = []
    for n, k in enumerate(ORDER):
        got_part = swap(parts[2 * n + 1], "c")
        total = shape((2, SHARD, HID), BF if k else F32)
        total = call(add_kernel, total, 2, 10**6, 2 * MIB, 4)(parts[2 * n], got_part)
        sums.append(shift(total, k) if k else total)
    token_grad = call(
        final_kernel, shape((SEQS, POS, D), BF), 3, 4 * 10**9, 16 * MIB, 32, specs=HBM, far=2,
        scratch=[
            pltpu.VMEM((16, 4, POS, D), BF),
            pltpu.VMEM((LANES, D), BF),
            pltpu.VMEM((SEQS, POS, D), BF),
            pltpu.SemaphoreType.DMA((9,)),
            pltpu.SemaphoreType.DMA((8,)),
        ],
    )(back, probs, mixing, in_hbm(rows), in_hbm(rxt))
    token_grad, *sums = lax.optimization_barrier((token_grad, *sums))
    grad = shape((1, SHARD, HID), F32)
    grad_in, grad_out = call(sum_kernel, (grad, grad), 4, 10**6, 4 * MIB, 6)(
        sums[3], sums[0], sums[1], sums[2]
    )
    return token_grad, grad_in, grad_out


def solution(mesh):
    fine = Mesh(mesh.devices.reshape(2, 4, 2, 4, 2), ("yh", "x", "c", "z", "yl"))
    dp, expert = ("yh", "x", "c"), ("z", "yl")
    seqs, weights = P(dp, expert, None), P(expert, dp, None)
    return jax.shard_map(
        on_device,
        mesh=fine,
        in_specs=(seqs, seqs, P(), weights, weights),
        out_specs=(P(None, expert + dp, None), weights, weights),
        check_vma=False,
    )
```

profile of v0, /device:TPU:0, one launch (start us, length us, event | category | flops | bytes accessed | tf_op | source)
XLA Modules:
  0.0 216.4 jit_solution(5737046502700702053)
XLA Ops:
  0.6 0.8 copy-done.4
  1.5 3.7 %pack.1 = (bf16[16,4,16,4096]{3,2,1,0:T(8,128)(2,1)S(1)}, bf16[2,256,512]{2,1,0:T(8,128)(2,1)S(1)}, bf16[128,4096]{1,0:T(8,128)(2,1)S(1)}) custom-call(bf16[2,16,16,4096]{3,2,1,0:T(8,128)(2,1)} %bitcast.5, bf16[2,16,16,4096]{3,2,1,0:T(8,128)(2,1)} %bitcast.6, bf16[1,256,512]{2,1,0:T(8,128)(2,1)} %wi_ref.1, bf16[1,256,512]{2,1,0:T(8,128)(2,1)} %wo_ref.1, ...), custom_call_target="tpu_custom_call" | custom-call | flops 8388608 | bytes 16777216 | tf_op jit(solution)/shard_map/pack/pallas_call | solution.py:73
  5.2 103.5 %all_to_all.15.a_ref.rows_ref = bf16[16,4,16,4096]{3,2,1,0:T(8,128)(2,1)S(1)} all-to-all(bf16[16,4,16,4096]{3,2,1,0:T(8,128)(2,1)S(1)} %get-tuple-element.30), channel_id=1, replica_groups=mesh['yh'=2,'x'=4,'c'=2,'z'=4,'yl'=2] {'yh','x','c'}, dimensions={0} | all-to-all | bytes 16777216 | tf_op jit(solution)/shard_map/all_to_all | solution.py:223
  108.7 4.1 %shard_map.76 = (bf16[2,8,2,16,2048]{4,3,2,1,0:T(8,128)(2,1)}, f32[512,128]{1,0:T(8,128)S(1)}, bf16[512,128]{1,0:T(8,128)(2,1)S(1)}) custom-call(bf16[16,4,16,4096]{3,2,1,0:T(8,128)(2,1)S(1)} %all_to_all.15.a_ref.rows_ref, bf16[128,4096]{1,0:T(8,128)(2,1)S(1)} %get-tuple-element.31.rxt_ref.far_rxt_ref), custom_call_target="tpu_custom_call" | custom-call | flops 3000000000 | bytes 12582912 | tf_op jit(solution)/shard_map/pallas_call | solution.py:224
  112.8 5.7 %all-to-all-start.1 = ((bf16[16,2,16,2048]{3,2,1,0:T(8,128)(2,1)}), bf16[16,2,16,2048]{3,2,1,0:T(8,128)(2,1)S(1)}, u32[]{:S(2)}, u32[]{:S(2)}) async-start(bf16[16,2,16,2048]{3,2,1,0:T(8,128)(2,1)} %bitcast.7), calls=%async_computation.1 | async-start | bytes 4194304 | tf_op jit(solution)/shard_map/all_to_all | solution.py:232
  118.5 0.8 collective-permute-start.5
  119.3 0.8 collective-permute-start.3
  120.1 0.7 collective-permute-start.1
  120.8 12.6 %collective-permute-done.5.refs_6_ = bf16[2,256,512]{2,1,0:T(8,128)(2,1)S(1)} collective-permute-done((bf16[2,256,512]{2,1,0:T(8,128)(2,1)S(1)}, bf16[2,256,512]{2,1,0:T(8,128)(2,1)S(1)}, u32[]{:S(2)}, u32[]{:S(2)}) %collective-permute-start.5) | collective-permute-done | bytes 524320 | tf_op jit(solution)/shard_map/ppermute | solution.py:214
  133.4 2.3 %collective-permute-done.3.refs_4_ = bf16[2,256,512]{2,1,0:T(8,128)(2,1)S(1)} collective-permute-done((bf16[2,256,512]{2,1,0:T(8,128)(2,1)S(1)}, bf16[2,256,512]{2,1,0:T(8,128)(2,1)S(1)}, u32[]{:S(2)}, u32[]{:S(2)}) %collective-permute-start.3) | collective-permute-done | bytes 524320 | tf_op jit(solution)/shard_map/ppermute | solution.py:214
  135.7 9.8 %collective-permute-done.1.refs_2_ = bf16[2,256,512]{2,1,0:T(8,128)(2,1)S(1)} collective-permute-done((bf16[2,256,512]{2,1,0:T(8,128)(2,1)S(1)}, bf16[2,256,512]{2,1,0:T(8,128)(2,1)S(1)}, u32[]{:S(2)}, u32[]{:S(2)}) %collective-permute-start.1) | collective-permute-done | bytes 524320 | tf_op jit(solution)/shard_map/ppermute | solution.py:214
  145.6 0.8 copy-done.7
  146.5 0.2 copy-done.9
  146.7 0.8 copy-done.10
  147.6 1.9 all-to-all-done.1.f_ref
  149.5 2.8 %shard_map.77 = (f32[2,256,512]{2,1,0:T(8,128)S(1)}, bf16[2,256,512]{2,1,0:T(8,128)(2,1)S(1)}, bf16[8,2,256,512]{3,2,1,0:T(8,128)(2,1)S(1)}) custom-call(bf16[16,2,16,2048]{3,2,1,0:T(8,128)(2,1)S(1)} %all-to-all-done.1.f_ref, bf16[2,256,512]{2,1,0:T(8,128)(2,1)} %copy-done.2, bf16[2,256,512]{2,1,0:T(8,128)(2,1)} %copy-done.8, ...), custom_call_target="tpu_custom_call" | custom-call | flops 1000000000 | bytes 8388608 | tf_op jit(solution)/shard_map/pallas_call | solution.py:240
  152.3 1.6 collective-permute-start.7
  153.9 12.6 %collective-permute-done.7.other_ref = bf16[2,256,512]{2,1,0:T(8,128)(2,1)S(1)} collective-permute-done((bf16[2,256,512]{2,1,0:T(8,128)(2,1)S(1)}, bf16[2,256,512]{2,1,0:T(8,128)(2,1)S(1)}, u32[]{:S(2)}, u32[]{:S(2)}) %collective-permute-start.7) | collective-permute-done | bytes 524320 | tf_op jit(solution)/shard_map/ppermute | solution.py:218
  166.6 2.1 shard_map.78
  168.7 6.5 %all-to-all-start.2 = ((bf16[16,2,16,2048]{3,2,1,0:T(8,128)(2,1)}), bf16[16,2,16,2048]{3,2,1,0:T(8,128)(2,1)}, u32[]{:S(2)}, u32[]{:S(2)}) async-start(bf16[16,2,16,2048]{3,2,1,0:T(8,128)(2,1)} %get-tuple-element.39), calls=%async_computation.2 | async-start | bytes 4194304 | tf_op jit(solution)/shard_map/all_to_all | solution.py:253
  175.3 1.3 shard_map.80
  176.7 0.5 collective-permute-start.10
  177.3 0.4 collective-permute-start.14
  177.7 0.9 collective-permute-done.8.got_ref
  178.6 0.1 shard_map.81
  178.7 1.4 collective-permute-start.9
  180.3 0.6 collective-permute-start.11
  180.9 0.9 shard_map.83
  181.9 2.7 %collective-permute-start.13 = (bf16[2,256,512]{2,1,0:T(8,128)(2,1)}, bf16[2,256,512]{2,1,0:T(8,128)(2,1)}, u32[]{:S(2)}, u32[]{:S(2)}) collective-permute-start(bf16[2,256,512]{2,1,0:T(8,128)(2,1)} %shard_map.83), channel_id=1, source_target_pairs={{0,48},{16,0},{32,16},{48,32},{1,49},{17,1},{33,17},{49,33},{2,50}... | collective-permute-start | bytes 1572872 | tf_op jit(solution)/shard_map/ppermute | solution.py:214
  184.6 21.2 %all-to-all-done.2.b_ref = bf16[16,2,16,2048]{3,2,1,0:T(8,128)(2,1)} async-done(((bf16[16,2,16,2048]{3,2,1,0:T(8,128)(2,1)}), bf16[16,2,16,2048]{3,2,1,0:T(8,128)(2,1)}, u32[]{:S(2)}, u32[]{:S(2)}) %all-to-all-start.2) | async-done | bytes 2097184 | tf_op jit(solution)/shard_map/all_to_all | solution.py:253
  205.8 8.5 %shard_map.79 = bf16[32,16,4096]{2,1,0:T(8,128)(2,1)} custom-call(bf16[16,2,16,2048]{3,2,1,0:T(8,128)(2,1)} %all-to-all-done.2.b_ref, f32[512,128]{1,0:T(8,128)S(1)} %get-tuple-element.40.probs_ref, bf16[512,128]{1,0:T(8,128)(2,1)S(1)} %get-tuple-element.34.mixing_ref, bf16[16,4,16,4096]{3,2,1,0:T(8,128)(2,1)} %copy-done, bf16[128,4096]{1,0:T(8,128)(2,1)} %copy-done.1), custom_call_target="tpu_custom_call" | custom-call | flops 4000000000 | bytes 16777216 | tf_op jit(solution)/shard_map/pallas_call | solution.py:263
  214.3 2.1 shard_map.85
  (36 shorter events, 0.7 us)
Async XLA Ops:
  0.6 0.8 copy-start.4
  5.1 103.6 %copy-start.2 = (bf16[2,256,512]{2,1,0:T(8,128)(2,1)}, bf16[2,256,512]{2,1,0:T(8,128)(2,1)S(1)}, u32[]{:S(2)}) copy-start(bf16[2,256,512]{2,1,0:T(8,128)(2,1)S(1)} %get-tuple-element.35.refs_0_) | copy-start | bytes 1572868
  5.2 103.6 %copy-start.1 = (bf16[128,4096]{1,0:T(8,128)(2,1)}, bf16[128,4096]{1,0:T(8,128)(2,1)S(1)}, u32[]{:S(2)}) copy-start(bf16[128,4096]{1,0:T(8,128)(2,1)S(1)} %get-tuple-element.31.rxt_ref.far_rxt_ref) | copy-start | bytes 3145732
  108.7 4.1 %copy-start = (bf16[16,4,16,4096]{3,2,1,0:T(8,128)(2,1)}, bf16[16,4,16,4096]{3,2,1,0:T(8,128)(2,1)S(1)}, u32[]{:S(2)}) copy-start(bf16[16,4,16,4096]{3,2,1,0:T(8,128)(2,1)S(1)} %all_to_all.15.a_ref.rows_ref) | copy-start | bytes 25165828
  112.8 5.7 %copy-start.3 = (bf16[2,256,512]{2,1,0:T(8,128)(2,1)S(1)}, bf16[2,256,512]{2,1,0:T(8,128)(2,1)}, u32[]{:S(2)}) copy-start(bf16[2,256,512]{2,1,0:T(8,128)(2,1)} %copy-done.2) | copy-start | bytes 1572868
  112.8 36.6 %all-to-all-start.1 = ((bf16[16,2,16,2048]{3,2,1,0:T(8,128)(2,1)}), bf16[16,2,16,2048]{3,2,1,0:T(8,128)(2,1)S(1)}, u32[]{:S(2)}, u32[]{:S(2)}) async-start(bf16[16,2,16,2048]{3,2,1,0:T(8,128)(2,1)} %bitcast.7), calls=%async_computation.1 | async-start | bytes 4194304 | tf_op jit(solution)/shard_map/all_to_all | solution.py:232
  118.5 14.9 %collective-permute-start.5 = (bf16[2,256,512]{2,1,0:T(8,128)(2,1)S(1)}, bf16[2,256,512]{2,1,0:T(8,128)(2,1)S(1)}, u32[]{:S(2)}, u32[]{:S(2)}) collective-permute-start(bf16[2,256,512]{2,1,0:T(8,128)(2,1)S(1)} %copy-done.3), channel_id=1, source_target_pairs={{0,48},{16,0},{32,16},{48,32},{1,49},{17,1},{33,17},{49,33},{2,50}... | collective-permute-start | bytes 1572872 | tf_op jit(solution)/shard_map/ppermute | solution.py:214
  119.3 16.3 %collective-permute-start.3 = (bf16[2,256,512]{2,1,0:T(8,128)(2,1)S(1)}, bf16[2,256,512]{2,1,0:T(8,128)(2,1)S(1)}, u32[]{:S(2)}, u32[]{:S(2)}) collective-permute-start(bf16[2,256,512]{2,1,0:T(8,128)(2,1)S(1)} %copy-done.3), channel_id=1, source_target_pairs={{0,32},{16,48},{32,0},{48,16},{1,33},{17,49},{33,1},{49,17},{2,34}... | collective-permute-start | bytes 1572872 | tf_op jit(solution)/shard_map/ppermute | solution.py:214
  120.1 25.4 %collective-permute-start.1 = (bf16[2,256,512]{2,1,0:T(8,128)(2,1)S(1)}, bf16[2,256,512]{2,1,0:T(8,128)(2,1)S(1)}, u32[]{:S(2)}, u32[]{:S(2)}) collective-permute-start(bf16[2,256,512]{2,1,0:T(8,128)(2,1)S(1)} %copy-done.3), channel_id=1, source_target_pairs={{0,16},{16,32},{32,48},{48,0},{1,17},{17,33},{33,49},{49,1},{2,18}... | collective-permute-start | bytes 1572872 | tf_op jit(solution)/shard_map/ppermute | solution.py:214
  120.8 24.8 %collective-permute-start = (bf16[2,256,512]{2,1,0:T(8,128)(2,1)S(1)}, bf16[2,256,512]{2,1,0:T(8,128)(2,1)S(1)}, u32[]{:S(2)}, u32[]{:S(2)}) collective-permute-start(bf16[2,256,512]{2,1,0:T(8,128)(2,1)S(1)} %copy-done.3), channel_id=1, source_target_pairs={{0,8},{8,0},{1,9},{9,1},{2,10},{10,2},{3,11},{11,3},{4,12},{12,4},... | collective-permute-start | bytes 1572872 | tf_op jit(solution)/shard_map/ppermute | solution.py:218
  133.4 16.1 %copy-start.5 = (bf16[2,256,512]{2,1,0:T(8,128)(2,1)}, bf16[2,256,512]{2,1,0:T(8,128)(2,1)S(1)}, u32[]{:S(2)}) copy-start(bf16[2,256,512]{2,1,0:T(8,128)(2,1)S(1)} %collective-permute-done.5.refs_6_) | copy-start | bytes 1572868
  133.4 12.2 %collective-permute-start.6 = (bf16[2,256,512]{2,1,0:T(8,128)(2,1)S(1)}, bf16[2,256,512]{2,1,0:T(8,128)(2,1)S(1)}, u32[]{:S(2)}, u32[]{:S(2)}) collective-permute-start(bf16[2,256,512]{2,1,0:T(8,128)(2,1)S(1)} %collective-permute-done.5.refs_6_), channel_id=1, source_target_pairs={{0,8},{8,0},{1,9},{9,1},{2,10},{10,2},{3,11},{11,3},{4,12},{12,4},... | collective-permute-start | bytes 1572872 | tf_op jit(solution)/shard_map/ppermute | solution.py:218
  135.7 9.9 %copy-start.6 = (bf16[2,256,512]{2,1,0:T(8,128)(2,1)}, bf16[2,256,512]{2,1,0:T(8,128)(2,1)S(1)}, u32[]{:S(2)}) copy-start(bf16[2,256,512]{2,1,0:T(8,128)(2,1)S(1)} %collective-permute-done.3.refs_4_) | copy-start | bytes 1572868
  135.7 9.9 %collective-permute-start.4 = (bf16[2,256,512]{2,1,0:T(8,128)(2,1)S(1)}, bf16[2,256,512]{2,1,0:T(8,128)(2,1)S(1)}, u32[]{:S(2)}, u32[]{:S(2)}) collective-permute-start(bf16[2,256,512]{2,1,0:T(8,128)(2,1)S(1)} %collective-permute-done.3.refs_4_), channel_id=1, source_target_pairs={{0,8},{8,0},{1,9},{9,1},{2,10},{10,2},{3,11},{11,3},{4,12},{12,4},... | collective-permute-start | bytes 1572872 | tf_op jit(solution)/shard_map/ppermute | solution.py:218
  145.5 0.8 copy-start.7
  145.5 2.0 collective-permute-start.2
  145.5 0.9 copy-start.8
  145.6 1.1 copy-start.9
  146.7 0.8 copy-start.10
  152.3 14.3 %collective-permute-start.7 = (bf16[2,256,512]{2,1,0:T(8,128)(2,1)S(1)}, bf16[2,256,512]{2,1,0:T(8,128)(2,1)S(1)}, u32[]{:S(2)}, u32[]{:S(2)}) collective-permute-start(bf16[2,256,512]{2,1,0:T(8,128)(2,1)S(1)} %get-tuple-element.37), channel_id=1, source_target_pairs={{0,64},{64,0},{1,65},{65,1},{2,66},{66,2},{3,67},{67,3},{4,68},{68... | collective-permute-start | bytes 1572872 | tf_op jit(solution)/shard_map/ppermute | solution.py:218
  168.7 37.0 %all-to-all-start.2 = ((bf16[16,2,16,2048]{3,2,1,0:T(8,128)(2,1)}), bf16[16,2,16,2048]{3,2,1,0:T(8,128)(2,1)}, u32[]{:S(2)}, u32[]{:S(2)}) async-start(bf16[16,2,16,2048]{3,2,1,0:T(8,128)(2,1)} %get-tuple-element.39), calls=%async_computation.2 | async-start | bytes 4194304 | tf_op jit(solution)/shard_map/all_to_all | solution.py:253
  176.6 2.0 collective-permute-start.8
  176.7 3.5 %collective-permute-start.10 = (bf16[2,256,512]{2,1,0:T(8,128)(2,1)S(1)}, bf16[2,256,512]{2,1,0:T(8,128)(2,1)S(1)}, u32[]{:S(2)}, u32[]{:S(2)}) collective-permute-start(bf16[2,256,512]{2,1,0:T(8,128)(2,1)S(1)} %get-tuple-element.45), channel_id=1, source_target_pairs={{0,8},{8,0},{1,9},{9,1},{2,10},{10,2},{3,11},{11,3},{4,12},{12,4},... | collective-permute-start | bytes 1572872 | tf_op jit(solution)/shard_map/ppermute | solution.py:218
  177.2 3.7 %collective-permute-start.12 = (bf16[2,256,512]{2,1,0:T(8,128)(2,1)S(1)}, bf16[2,256,512]{2,1,0:T(8,128)(2,1)S(1)}, u32[]{:S(2)}, u32[]{:S(2)}) collective-permute-start(bf16[2,256,512]{2,1,0:T(8,128)(2,1)S(1)} %get-tuple-element.47), channel_id=1, source_target_pairs={{0,8},{8,0},{1,9},{9,1},{2,10},{10,2},{3,11},{11,3},{4,12},{12,4},... | collective-permute-start | bytes 1572872 | tf_op jit(solution)/shard_map/ppermute | solution.py:218
  177.3 7.2 %collective-permute-start.14 = (bf16[2,256,512]{2,1,0:T(8,128)(2,1)S(1)}, bf16[2,256,512]{2,1,0:T(8,128)(2,1)S(1)}, u32[]{:S(2)}, u32[]{:S(2)}) collective-permute-start(bf16[2,256,512]{2,1,0:T(8,128)(2,1)S(1)} %get-tuple-element.49), channel_id=1, source_target_pairs={{0,8},{8,0},{1,9},{9,1},{2,10},{10,2},{3,11},{11,3},{4,12},{12,4},... | collective-permute-start | bytes 1572872 | tf_op jit(solution)/shard_map/ppermute | solution.py:218
  178.7 35.6 %collective-permute-start.9 = (bf16[2,256,512]{2,1,0:T(8,128)(2,1)S(1)}, bf16[2,256,512]{2,1,0:T(8,128)(2,1)S(1)}, u32[]{:S(2)}, u32[]{:S(2)}) collective-permute-start(bf16[2,256,512]{2,1,0:T(8,128)(2,1)S(1)} %shard_map.81), channel_id=1, source_target_pairs={{0,32},{16,48},{32,0},{48,16},{1,33},{17,49},{33,1},{49,17},{2,34}... | collective-permute-start | bytes 1572872 | tf_op jit(solution)/shard_map/ppermute | solution.py:214
  180.3 34.0 %collective-permute-start.11 = (bf16[2,256,512]{2,1,0:T(8,128)(2,1)S(1)}, bf16[2,256,512]{2,1,0:T(8,128)(2,1)S(1)}, u32[]{:S(2)}, u32[]{:S(2)}) collective-permute-start(bf16[2,256,512]{2,1,0:T(8,128)(2,1)S(1)} %shard_map.82), channel_id=1, source_target_pairs={{0,16},{16,32},{32,48},{48,0},{1,17},{17,33},{33,49},{49,1},{2,18}... | collective-permute-start | bytes 1572872 | tf_op jit(solution)/shard_map/ppermute | solution.py:214
  181.9 32.5 %collective-permute-start.13 = (bf16[2,256,512]{2,1,0:T(8,128)(2,1)}, bf16[2,256,512]{2,1,0:T(8,128)(2,1)}, u32[]{:S(2)}, u32[]{:S(2)}) collective-permute-start(bf16[2,256,512]{2,1,0:T(8,128)(2,1)} %shard_map.83), channel_id=1, source_target_pairs={{0,48},{16,0},{32,16},{48,32},{1,49},{17,1},{33,17},{49,33},{2,50}... | collective-permute-start | bytes 1572872 | tf_op jit(solution)/shard_map/ppermute | solution.py:214
where the time goes:
time: 217 us; the launch traced here: 216 us
  blocking collectives  104 us (48%)
  waiting for transfers between devices  61.4 us (28%)
  Pallas kernels  25.9 us (12%)
  starting transfers between devices  21.9 us (10%)
  local copies, waits for them, and re-layouts  2.77 us (1%)
    all_to_all x1, blocking collectives, on_device(): rows = lax.all_to_all(rows, ('yh', 'x', 'c'), 0, 0, tiled=True)  104 us
    ppermute x6, waiting for transfers between devices, shift(): return lax.ppermute(x, 'x', [(i, (i + k) % 4) for i in range(4)])  24.7 us
    all_to_all x1, waiting for transfers between devices, on_device(): back = lax.all_to_all(back, experts, 0, 0, tiled=True)  21.2 us
    ppermute x9, waiting for transfers between devices, swap(): return lax.ppermute(x, axis, [(0, 1), (1, 0)])  13.6 us
    pallas_call x1, Pallas kernels, on_device(): call(final_kernel, shape((SEQS, POS, D), BF), 3, 4 * 10 ** 9, 16 * MIB, 3...  8.51 us
    ppermute x6, starting transfers between devices, shift(): return lax.ppermute(x, 'x', [(i, (i + k) % 4) for i in range(4)])  6.99 us
    all_to_all x1, starting transfers between devices, on_device(): back = lax.all_to_all(back, experts, 0, 0, tiled=True)  6.54 us
    all_to_all x1, starting transfers between devices, on_device(): lax.all_to_all(mixed.reshape(16, 2, POS, HALF), experts, 0, 0, tiled=True)  5.68 us
  transfers between devices with their start and end apart: 17, of which 8 were waited for; matrix products, arithmetic and copies ran while one was open for 0% of the time, Pallas kernels for 5%

commit v1 on v0

--- a/solution.py
+++ b/solution.py
@@ -1,3 +1,5 @@
+import functools
+
 import jax
 import jax.numpy as jnp
 from jax import lax
@@ -51,17 +53,20 @@
     return lax.dot_general(a, b, (((0,), (0,)), ((), ())), preferred_element_type=F32)
 
 
-def pack_kernel(t_ref, g_ref, wi_ref, wo_ref, router_ref, o_ref, w_ref, rxt_ref, sem):
+def pack_kernel(t_ref, g_ref, wi_ref, wo_ref, router_ref, o_ref, w_ref, rxt_ref, few, sem):
     copies = []
     for i in range(16):
         src, seq, part = (t_ref, g_ref)[i // 8], i // 4 % 2, pl.ds(i % 4 * 4, 4)
         copies.append(pltpu.make_async_copy(src.at[seq, part], o_ref.at[part, i // 4], sem.at[i]))
     copies.append(pltpu.make_async_copy(wi_ref.at[0], w_ref.at[0], sem.at[16]))
     copies.append(pltpu.make_async_copy(wo_ref.at[0], w_ref.at[1], sem.at[17]))
+    scores = pltpu.make_async_copy(router_ref, few, sem.at[18])
+    scores.start()
     for copy in copies:
         copy.start()
+    scores.wait()
     for e in range(EXPERTS):
-        row = router_ref[e : e + 1, :].astype(F32)
+        row = few[e : e + 1, :].astype(F32)
         rxt_ref[e * POS : (e + 1) * POS, :] = jnp.broadcast_to(row, (POS, D)).astype(BF)
     for copy in copies:
         copy.wait()
@@ -69,17 +74,17 @@
 
 def pack(tokens, out_grad, weight_in, weight_out, router):
     blocks = (2, 16, POS, D)
-    arrays = (tokens.reshape(blocks), out_grad.reshape(blocks), weight_in, weight_out)
+    arrays = (tokens.reshape(blocks), out_grad.reshape(blocks), weight_in, weight_out, router.T)
     return pl.pallas_call(
         pack_kernel,
         out_shape=(shape((16, 4, POS, D), BF), shape((2, SHARD, HID), BF), shape((LANES, D), BF)),
-        in_specs=[HBM] * 4 + [VM],
+        in_specs=[HBM] * 5,
         out_specs=(VM, VM, VM),
-        scratch_shapes=[pltpu.SemaphoreType.DMA((18,))],
+        scratch_shapes=[pltpu.VMEM((EXPERTS, D), BF), pltpu.SemaphoreType.DMA((19,))],
         cost_estimate=pl.CostEstimate(flops=8 * MIB, bytes_accessed=16 * MIB, transcendentals=0),
         compiler_params=pltpu.CompilerParams(vmem_limit_bytes=16 * MIB),
         name="pack",
-    )(*[in_hbm(a) for a in arrays], router.T)
+    )(*[in_hbm(a) for a in arrays])
 
 
 def own_position():
@@ -120,50 +125,57 @@
     return pl.ds(pl.multiple_of(owner * SHARD, SHARD), SHARD)
 
 
-def partial_kernel(f_ref, *refs):
+def partial_kernel(t, f_ref, *refs):
     shard_refs, (own_ref, send_ref, w_ref, sem) = refs[:8], refs[8:]
-    copies = [pltpu.make_async_copy(ref, w_ref.at[i], sem.at[i]) for i, ref in enumerate(shard_refs)]
+    copies = [pltpu.make_async_copy(ref.at[t], w_ref.at[i], sem.at[i]) for i, ref in enumerate(shard_refs)]
     for copy in copies:
         copy.start()
-    sums = [jnp.zeros((256, HID), F32) for _ in range(2)]
+    total = jnp.zeros((256, HID), F32)
     for i, copy in enumerate(copies):
         cols = shard_columns(i // 2, i % 2)
         copy.wait()
-        for t in range(2):
-            block = f_ref[:, t, :, cols].reshape(256, SHARD)
-            sums[t] += jnp.dot(block, w_ref[i, t], preferred_element_type=F32)
-    for t in range(2):
-        own_ref[t] = sums[t]
-        send_ref[t] = sums[t].astype(BF)
-
-
-def expert_kernel(own_ref, other_ref, w_ref, b_ref, hidden_ref, held, sem):
-    pre = own_ref[0] + other_ref[0].astype(F32)
-    hidden_full = own_ref[1] + other_ref[1].astype(F32)
-    sigma = jax.nn.sigmoid(pre)
-    hidden = (pre * sigma).astype(BF)
-    hidden_grad = (hidden_full * sigma * (1.0 + pre * (1.0 - sigma))).astype(BF)
-    hidden_ref[0] = hidden_grad
-    hidden_ref[1] = hidden
-    copies = []
+        block = f_ref[:, t, :, cols].reshape(256, SHARD)
+        total += jnp.dot(block, w_ref[i], preferred_element_type=F32)
+    own_ref[...] = total
+    send_ref[...] = total.astype(BF)
+
+
+def forward_kernel(own_ref, other_ref, w_ref, out_ref, pre_ref, hidden_ref):
+    pre = own_ref[...] + other_ref[...].astype(F32)
+    pre_ref[...] = pre
+    hidden = (pre * jax.nn.sigmoid(pre)).astype(BF)
+    hidden_ref[...] = hidden
     for i in range(8):
         cols = shard_columns(i // 2, i % 2)
-        held[:, 0, :, cols] = nt(hidden, w_ref[i, 1]).astype(BF).reshape(16, POS, SHARD)
-        held[:, 1, :, cols] = nt(hidden_grad, w_ref[i, 0]).astype(BF).reshape(16, POS, SHARD)
-        place = (slice(None), slice(None), slice(None), cols)
-        copies.append(pltpu.make_async_copy(held.at[place], b_ref.at[place], sem.at[i]))
-        copies[i].start()
-    for copy in copies:
-        copy.wait()
-
-
-def grads_kernel(f_ref, hidden_ref, *out_refs):
+        out_ref[:, :, cols] = nt(hidden, w_ref[i]).astype(BF).reshape(16, POS, SHARD)
+
+
+def backward_kernel(own_ref, other_ref, pre_ref, w_ref, out_ref, b_ref, hidden_grad_ref, held, sem):
+    copies = [pltpu.make_async_copy(out_ref, b_ref.at[:, 0], sem.at[2])]
+    copies[0].start()
+    pre = pre_ref[...]
+    sigma = jax.nn.sigmoid(pre)
+    hidden_full = own_ref[...] + other_ref[...].astype(F32)
+    hidden_grad = (hidden_full * sigma * (1.0 + pre * (1.0 - sigma))).astype(BF)
+    hidden_grad_ref[...] = hidden_grad
+    for r in range(2):
+        part = pl.ds(8 * r, 8)
+        for i in range(8):
+            block = nt(hidden_grad[128 * r : 128 * r + 128], w_ref[i])
+            held[part, :, shard_columns(i // 2, i % 2)] = block.astype(BF).reshape(8, POS, SHARD)
+        copies.append(pltpu.make_async_copy(held.at[part], b_ref.at[part, 1], sem.at[r]))
+        copies[-1].start()
+    for copy in copies:
+        copy.wait()
+
+
+def grads_kernel(f_ref, hidden_grad_ref, hidden_ref, *out_refs):
     for n, k in enumerate(ORDER):
         for j in range(2):
             cols = shard_columns(4 - k, j)
-            for t in range(2):
+            for t, ref in enumerate((hidden_grad_ref, hidden_ref)):
                 block = f_ref[:, t, :, cols].reshape(256, SHARD)
-                out_refs[2 * n + j][t] = tn(block, hidden_ref[t]).astype(BF)
+                out_refs[2 * n + j][t] = tn(block, ref[...]).astype(BF)
 
 
 def add_kernel(keep_ref, got_ref, o_ref):
@@ -237,29 +249,35 @@
     for w in shards:
         weights += [w, swap(w, "c")]
 
-    own, send, weights = call(
-        partial_kernel,
-        (shape((2, 256, HID), F32), shape((2, 256, HID), BF), shape((8, 2, SHARD, HID), BF)),
-        1, 10**9, 8 * MIB, 14, far=8,
-        scratch=[pltpu.SemaphoreType.DMA((8,))],
-    )(got, *[in_hbm(w) for w in weights])
-    other = swap(send, "yh")
-    back, hidden = call(
-        expert_kernel,
-        (pltpu.HBM((16, 2, POS, HALF), BF), shape((2, 256, HID), BF)),
-        3, 10**9, 8 * MIB, 16, specs=(HBM, VM),
-        scratch=[pltpu.VMEM((16, 2, POS, HALF), BF), pltpu.SemaphoreType.DMA((8,))],
-    )(own, other, weights)
+    far_weights = [in_hbm(w) for w in weights]
+    wide, narrow = shape((256, HID), F32), shape((256, HID), BF)
+    owns, others, weights = [], [], []
+    for t in range(2):
+        own, send, w = call(
+            functools.partial(partial_kernel, t), (wide, narrow, shape((8, SHARD, HID), BF)),
+            1, 10**9, 4 * MIB, 10, far=8, scratch=[pltpu.SemaphoreType.DMA((8,))],
+        )(got, *far_weights)
+        owns.append(own)
+        weights.append(w)
+        others.append(swap(send, "yh"))
+    out, pre, hidden = call(
+        forward_kernel, (shape((16, POS, HALF), BF), wide, narrow), 3, 10**9, 4 * MIB, 10,
+    )(owns[0], others[0], weights[1])
+    back, hidden_grad = call(
+        backward_kernel, (pltpu.HBM((16, 2, POS, HALF), BF), narrow),
+        5, 10**9, 4 * MIB, 10, specs=(HBM, VM),
+        scratch=[pltpu.VMEM((16, POS, HALF), BF), pltpu.SemaphoreType.DMA((3,))],
+    )(owns[1], others[1], pre, weights[0], out)
     back = lax.all_to_all(back, experts, 0, 0, tiled=True)
 
     piece = shape((2, SHARD, HID), BF)
-    parts = call(grads_kernel, (piece,) * 8, 2, 10**9, 8 * MIB, 14)(got, hidden)
+    parts = call(grads_kernel, (piece,) * 8, 3, 10**9, 8 * MIB, 14)(got, hidden_grad, hidden)
     sums = []
     for n, k in enumerate(ORDER):
         got_part = swap(parts[2 * n + 1], "c")
         total = shape((2, SHARD, HID), BF if k else F32)
-        total = call(add_kernel, total, 2, 10**6, 2 * MIB, 4)(parts[2 * n], got_part)
-        sums.append(shift(total, k) if k else total)
+        sums.append(call(add_kernel, total, 2, 10**6, 2 * MIB, 4)(parts[2 * n], got_part))
+    sums = [shift(x, k) if k else x for x, k in zip(sums, ORDER)]
     token_grad = call(
         final_kernel, shape((SEQS, POS, D), BF), 3, 4 * 10**9, 16 * MIB, 32, specs=HBM, far=2,
         scratch=[

time: 217 us -> 215 us (level)
  waiting for transfers between devices: 61.4 us -> 56.5 us
  Pallas kernels: 25.9 us -> 28.2 us
    ppermute x9 -> x10, waiting for transfers between devices: 13.6 us -> 8.69 us  [swap(): return lax.ppermute(x, axis, [(0, 1), (1, 0)])]
    pallas_call x3 -> x5, Pallas kernels: 6.32 us -> 8.57 us  [the longest x2 4.14 us: on_device(): call(functools.partial(partial_kernel, t), (wide, narrow, shape((8, SHARD...]
    ppermute x9 -> x10, starting transfers between devices: 2.73 us -> 4.81 us  [swap(): return lax.ppermute(x, axis, [(0, 1), (1, 0)])]
  transfers between devices with their start and end apart: 17 -> 18, of which waited for: 8 -> 9; matrix products, arithmetic and copies ran while one was open for 0% -> 0% of each run, Pallas kernels for 5% -> 6%
where the time goes in v1:
time: 215 us
  blocking collectives  104 us (48%)
  waiting for transfers between devices  56.5 us (26%)
  Pallas kernels  28.2 us (13%)
  starting transfers between devices  23.8 us (11%)
    all_to_all x1, blocking collectives, on_device(): rows = lax.all_to_all(rows, ('yh', 'x', 'c'), 0, 0, tiled=True)  104 us
    ppermute x6, waiting for transfers between devices, shift(): return lax.ppermute(x, 'x', [(i, (i + k) % 4) for i in range(4)])  24.7 us
    all_to_all x1, waiting for transfers between devices, on_device(): back = lax.all_to_all(back, experts, 0, 0, tiled=True)  21.1 us
    ppermute x10, waiting for transfers between devices, swap(): return lax.ppermute(x, axis, [(0, 1), (1, 0)])  8.69 us
    pallas_call x1, Pallas kernels, on_device(): call(final_kernel, shape((SEQS, POS, D), BF), 3, 4 * 10 ** 9, 16 * MIB, 3...  8.51 us
    ppermute x6, starting transfers between devices, shift(): return lax.ppermute(x, 'x', [(i, (i + k) % 4) for i in range(4)])  7.01 us
    all_to_all x1, starting transfers between devices, on_device(): back = lax.all_to_all(back, experts, 0, 0, tiled=True)  6.46 us
    all_to_all x1, starting transfers between devices, on_device(): lax.all_to_all(mixed.reshape(16, 2, POS, HALF), experts, 0, 0, tiled=True)  5.54 us
  transfers between devices with their start and end apart: 18, of which 9 were waited for; matrix products, arithmetic and copies ran while one was open for 0% of the time, Pallas kernels for 6%

profile of v1, /device:TPU:0, one launch (start us, length us, event | category | flops | bytes accessed | tf_op | source)
XLA Modules:
  0.0 214.8 jit_solution(1368989325267986380)
XLA Ops:
  0.6 3.7 %pack.1 = (bf16[16,4,16,4096]{3,2,1,0:T(8,128)(2,1)S(1)}, bf16[2,256,512]{2,1,0:T(8,128)(2,1)S(1)}, bf16[128,4096]{1,0:T(8,128)(2,1)S(1)}) custom-call(bf16[2,16,16,4096]{3,2,1,0:T(8,128)(2,1)} %bitcast.4, bf16[2,16,16,4096]{3,2,1,0:T(8,128)(2,1)} %bitcast.5, bf16[1,256,512]{2,1,0:T(8,128)(2,1)} %wi_ref.1, bf16[1,256,512]{2,1,0:T(8,128)(2,1)} %wo_ref.1, ...), custom_call_target="tpu_custom_call" | custom-call | flops 8388608 | bytes 16777216 | tf_op jit(solution)/shard_map/pack/pallas_call | solution.py:78
  4.4 103.5 %all_to_all.15.a_ref.rows_ref = bf16[16,4,16,4096]{3,2,1,0:T(8,128)(2,1)S(1)} all-to-all(bf16[16,4,16,4096]{3,2,1,0:T(8,128)(2,1)S(1)} %get-tuple-element.36), channel_id=1, replica_groups=mesh['yh'=2,'x'=4,'c'=2,'z'=4,'yl'=2] {'yh','x','c'}, dimensions={0} | all-to-all | bytes 16777216 | tf_op jit(solution)/shard_map/all_to_all | solution.py:235
  107.9 4.1 %shard_map.76 = (bf16[2,8,2,16,2048]{4,3,2,1,0:T(8,128)(2,1)}, f32[512,128]{1,0:T(8,128)S(1)}, bf16[512,128]{1,0:T(8,128)(2,1)S(1)}) custom-call(bf16[16,4,16,4096]{3,2,1,0:T(8,128)(2,1)S(1)} %all_to_all.15.a_ref.rows_ref, bf16[128,4096]{1,0:T(8,128)(2,1)S(1)} %get-tuple-element.37.rxt_ref.far_rxt_ref), custom_call_target="tpu_custom_call" | custom-call | flops 3000000000 | bytes 12582912 | tf_op jit(solution)/shard_map/pallas_call | solution.py:236
  112.0 5.5 %all-to-all-start.1 = ((bf16[16,2,16,2048]{3,2,1,0:T(8,128)(2,1)}), bf16[16,2,16,2048]{3,2,1,0:T(8,128)(2,1)S(1)}, u32[]{:S(2)}, u32[]{:S(2)}) async-start(bf16[16,2,16,2048]{3,2,1,0:T(8,128)(2,1)} %bitcast.6), calls=%async_computation.1 | async-start | bytes 4194304 | tf_op jit(solution)/shard_map/all_to_all | solution.py:244
  117.6 0.8 collective-permute-start.5
  118.4 0.8 collective-permute-start.3
  119.2 0.7 collective-permute-start.1
  119.8 12.6 %collective-permute-done.5.refs_6_ = bf16[2,256,512]{2,1,0:T(8,128)(2,1)S(1)} collective-permute-done((bf16[2,256,512]{2,1,0:T(8,128)(2,1)S(1)}, bf16[2,256,512]{2,1,0:T(8,128)(2,1)S(1)}, u32[]{:S(2)}, u32[]{:S(2)}) %collective-permute-start.5) | collective-permute-done | bytes 524320 | tf_op jit(solution)/shard_map/ppermute | solution.py:226
  132.4 2.3 %collective-permute-done.3.refs_4_ = bf16[2,256,512]{2,1,0:T(8,128)(2,1)S(1)} collective-permute-done((bf16[2,256,512]{2,1,0:T(8,128)(2,1)S(1)}, bf16[2,256,512]{2,1,0:T(8,128)(2,1)S(1)}, u32[]{:S(2)}, u32[]{:S(2)}) %collective-permute-start.3) | collective-permute-done | bytes 524320 | tf_op jit(solution)/shard_map/ppermute | solution.py:226
  134.7 9.8 %collective-permute-done.1.refs_2_ = bf16[2,256,512]{2,1,0:T(8,128)(2,1)S(1)} collective-permute-done((bf16[2,256,512]{2,1,0:T(8,128)(2,1)S(1)}, bf16[2,256,512]{2,1,0:T(8,128)(2,1)S(1)}, u32[]{:S(2)}, u32[]{:S(2)}) %collective-permute-start.1) | collective-permute-done | bytes 524320 | tf_op jit(solution)/shard_map/ppermute | solution.py:226
  144.6 0.8 copy-done.5
  145.7 0.8 copy-done.8
  146.6 1.9 all-to-all-done.1.f_ref
  148.5 2.1 shard_map.78
  150.6 1.6 collective-permute-start.8
  152.2 2.1 shard_map.77
  154.3 2.1 collective-permute-start.7
  156.4 4.0 %collective-permute-done.8.other_ref = bf16[256,512]{1,0:T(8,128)(2,1)S(1)} collective-permute-done((bf16[256,512]{1,0:T(8,128)(2,1)S(1)}, bf16[256,512]{1,0:T(8,128)(2,1)S(1)}, u32[]{:S(2)}, u32[]{:S(2)}) %collective-permute-start.8) | collective-permute-done | bytes 262176 | tf_op jit(solution)/shard_map/ppermute | solution.py:230
  160.4 0.8 shard_map.79
  161.2 3.7 %collective-permute-done.7.other_ref = bf16[256,512]{1,0:T(8,128)(2,1)S(1)} collective-permute-done((bf16[256,512]{1,0:T(8,128)(2,1)S(1)}, bf16[256,512]{1,0:T(8,128)(2,1)S(1)}, u32[]{:S(2)}, u32[]{:S(2)}) %collective-permute-start.7) | collective-permute-done | bytes 262176 | tf_op jit(solution)/shard_map/ppermute | solution.py:230
  164.9 2.3 %shard_map.80 = (bf16[16,2,16,2048]{3,2,1,0:T(8,128)(2,1)}, bf16[256,512]{1,0:T(8,128)(2,1)S(1)}) custom-call(f32[256,512]{1,0:T(8,128)S(1)} %get-tuple-element.42.own_ref, bf16[256,512]{1,0:T(8,128)(2,1)S(1)} %collective-permute-done.7.other_ref, f32[256,512]{1,0:T(8,128)S(1)} %get-tuple-element.47.pre_ref, ...), custom_call_target="tpu_custom_call" | custom-call | flops 1000000000 | bytes 4194304 | tf_op jit(solution)/shard_map/pallas_call | solution.py:266
  167.2 6.5 %all-to-all-start.2 = ((bf16[16,2,16,2048]{3,2,1,0:T(8,128)(2,1)}), bf16[16,2,16,2048]{3,2,1,0:T(8,128)(2,1)}, u32[]{:S(2)}, u32[]{:S(2)}) async-start(bf16[16,2,16,2048]{3,2,1,0:T(8,128)(2,1)} %get-tuple-element.50), calls=%async_computation.2 | async-start | bytes 4194304 | tf_op jit(solution)/shard_map/all_to_all | solution.py:271
  173.7 1.3 shard_map.82
  175.1 0.5 collective-permute-start.11
  176.1 0.9 collective-permute-done.9.got_ref
  177.1 1.4 collective-permute-start.10
  178.7 0.6 collective-permute-start.12
  179.3 0.9 shard_map.85
  180.2 2.7 %collective-permute-start.14 = (bf16[2,256,512]{2,1,0:T(8,128)(2,1)}, bf16[2,256,512]{2,1,0:T(8,128)(2,1)}, u32[]{:S(2)}, u32[]{:S(2)}) collective-permute-start(bf16[2,256,512]{2,1,0:T(8,128)(2,1)} %shard_map.85), channel_id=1, source_target_pairs={{0,48},{16,0},{32,16},{48,32},{1,49},{17,1},{33,17},{49,33},{2,50}... | collective-permute-start | bytes 1572872 | tf_op jit(solution)/shard_map/ppermute | solution.py:226
  183.0 21.1 %all-to-all-done.2.b_ref = bf16[16,2,16,2048]{3,2,1,0:T(8,128)(2,1)} async-done(((bf16[16,2,16,2048]{3,2,1,0:T(8,128)(2,1)}), bf16[16,2,16,2048]{3,2,1,0:T(8,128)(2,1)}, u32[]{:S(2)}, u32[]{:S(2)}) %all-to-all-start.2) | async-done | bytes 2097184 | tf_op jit(solution)/shard_map/all_to_all | solution.py:271
  204.1 8.5 %shard_map.81 = bf16[32,16,4096]{2,1,0:T(8,128)(2,1)} custom-call(bf16[16,2,16,2048]{3,2,1,0:T(8,128)(2,1)} %all-to-all-done.2.b_ref, f32[512,128]{1,0:T(8,128)S(1)} %get-tuple-element.51.probs_ref, bf16[512,128]{1,0:T(8,128)(2,1)S(1)} %get-tuple-element.40.mixing_ref, bf16[16,4,16,4096]{3,2,1,0:T(8,128)(2,1)} %copy-done, bf16[128,4096]{1,0:T(8,128)(2,1)} %copy-done.2), custom_call_target="tpu_custom_call" | custom-call | flops 4000000000 | bytes 16777216 | tf_op jit(solution)/shard_map/pallas_call | solution.py:281
  212.7 2.1 shard_map.87
  (36 shorter events, 1.4 us)
Async XLA Ops:
  4.3 103.6 %copy-start.2 = (bf16[128,4096]{1,0:T(8,128)(2,1)}, bf16[128,4096]{1,0:T(8,128)(2,1)S(1)}, u32[]{:S(2)}) copy-start(bf16[128,4096]{1,0:T(8,128)(2,1)S(1)} %get-tuple-element.37.rxt_ref.far_rxt_ref) | copy-start | bytes 3145732
  4.4 115.5 %copy-start.1 = (bf16[2,256,512]{2,1,0:T(8,128)(2,1)}, bf16[2,256,512]{2,1,0:T(8,128)(2,1)S(1)}, u32[]{:S(2)}) copy-start(bf16[2,256,512]{2,1,0:T(8,128)(2,1)S(1)} %get-tuple-element.41.refs_0_) | copy-start | bytes 1572868
  107.9 4.1 %copy-start = (bf16[16,4,16,4096]{3,2,1,0:T(8,128)(2,1)}, bf16[16,4,16,4096]{3,2,1,0:T(8,128)(2,1)S(1)}, u32[]{:S(2)}) copy-start(bf16[16,4,16,4096]{3,2,1,0:T(8,128)(2,1)S(1)} %all_to_all.15.a_ref.rows_ref) | copy-start | bytes 25165828
  112.0 36.5 %all-to-all-start.1 = ((bf16[16,2,16,2048]{3,2,1,0:T(8,128)(2,1)}), bf16[16,2,16,2048]{3,2,1,0:T(8,128)(2,1)S(1)}, u32[]{:S(2)}, u32[]{:S(2)}) async-start(bf16[16,2,16,2048]{3,2,1,0:T(8,128)(2,1)} %bitcast.6), calls=%async_computation.1 | async-start | bytes 4194304 | tf_op jit(solution)/shard_map/all_to_all | solution.py:244
  117.6 14.9 %collective-permute-start.5 = (bf16[2,256,512]{2,1,0:T(8,128)(2,1)S(1)}, bf16[2,256,512]{2,1,0:T(8,128)(2,1)S(1)}, u32[]{:S(2)}, u32[]{:S(2)}) collective-permute-start(bf16[2,256,512]{2,1,0:T(8,128)(2,1)S(1)} %get-tuple-element.41.refs_0_), channel_id=1, source_target_pairs={{0,48},{16,0},{32,16},{48,32},{1,49},{17,1},{33,17},{49,33},{2,50}... | collective-permute-start | bytes 1572872 | tf_op jit(solution)/shard_map/ppermute | solution.py:226
  118.4 16.3 %collective-permute-start.3 = (bf16[2,256,512]{2,1,0:T(8,128)(2,1)S(1)}, bf16[2,256,512]{2,1,0:T(8,128)(2,1)S(1)}, u32[]{:S(2)}, u32[]{:S(2)}) collective-permute-start(bf16[2,256,512]{2,1,0:T(8,128)(2,1)S(1)} %get-tuple-element.41.refs_0_), channel_id=1, source_target_pairs={{0,32},{16,48},{32,0},{48,16},{1,33},{17,49},{33,1},{49,17},{2,34}... | collective-permute-start | bytes 1572872 | tf_op jit(solution)/shard_map/ppermute | solution.py:226
  119.2 25.4 %collective-permute-start.1 = (bf16[2,256,512]{2,1,0:T(8,128)(2,1)S(1)}, bf16[2,256,512]{2,1,0:T(8,128)(2,1)S(1)}, u32[]{:S(2)}, u32[]{:S(2)}) collective-permute-start(bf16[2,256,512]{2,1,0:T(8,128)(2,1)S(1)} %get-tuple-element.41.refs_0_), channel_id=1, source_target_pairs={{0,16},{16,32},{32,48},{48,0},{1,17},{17,33},{33,49},{49,1},{2,18}... | collective-permute-start | bytes 1572872 | tf_op jit(solution)/shard_map/ppermute | solution.py:226
  119.8 24.8 %collective-permute-start = (bf16[2,256,512]{2,1,0:T(8,128)(2,1)S(1)}, bf16[2,256,512]{2,1,0:T(8,128)(2,1)S(1)}, u32[]{:S(2)}, u32[]{:S(2)}) collective-permute-start(bf16[2,256,512]{2,1,0:T(8,128)(2,1)S(1)} %get-tuple-element.41.refs_0_), channel_id=1, source_target_pairs={{0,8},{8,0},{1,9},{9,1},{2,10},{10,2},{3,11},{11,3},{4,12},{12,4},... | collective-permute-start | bytes 1572872 | tf_op jit(solution)/shard_map/ppermute | solution.py:230
  132.4 16.1 %copy-start.3 = (bf16[2,256,512]{2,1,0:T(8,128)(2,1)}, bf16[2,256,512]{2,1,0:T(8,128)(2,1)S(1)}, u32[]{:S(2)}) copy-start(bf16[2,256,512]{2,1,0:T(8,128)(2,1)S(1)} %collective-permute-done.5.refs_6_) | copy-start | bytes 1572868
  132.4 12.2 %collective-permute-start.6 = (bf16[2,256,512]{2,1,0:T(8,128)(2,1)S(1)}, bf16[2,256,512]{2,1,0:T(8,128)(2,1)S(1)}, u32[]{:S(2)}, u32[]{:S(2)}) collective-permute-start(bf16[2,256,512]{2,1,0:T(8,128)(2,1)S(1)} %collective-permute-done.5.refs_6_), channel_id=1, source_target_pairs={{0,8},{8,0},{1,9},{9,1},{2,10},{10,2},{3,11},{11,3},{4,12},{12,4},... | collective-permute-start | bytes 1572872 | tf_op jit(solution)/shard_map/ppermute | solution.py:230
  134.7 9.9 %copy-start.4 = (bf16[2,256,512]{2,1,0:T(8,128)(2,1)}, bf16[2,256,512]{2,1,0:T(8,128)(2,1)S(1)}, u32[]{:S(2)}) copy-start(bf16[2,256,512]{2,1,0:T(8,128)(2,1)S(1)} %collective-permute-done.3.refs_4_) | copy-start | bytes 1572868
  134.7 9.9 %collective-permute-start.4 = (bf16[2,256,512]{2,1,0:T(8,128)(2,1)S(1)}, bf16[2,256,512]{2,1,0:T(8,128)(2,1)S(1)}, u32[]{:S(2)}, u32[]{:S(2)}) collective-permute-start(bf16[2,256,512]{2,1,0:T(8,128)(2,1)S(1)} %collective-permute-done.3.refs_4_), channel_id=1, source_target_pairs={{0,8},{8,0},{1,9},{9,1},{2,10},{10,2},{3,11},{11,3},{4,12},{12,4},... | collective-permute-start | bytes 1572872 | tf_op jit(solution)/shard_map/ppermute | solution.py:230
  144.6 0.8 copy-start.5
  144.6 2.0 collective-permute-start.2
  144.6 0.9 copy-start.6
  144.6 1.1 copy-start.7
  145.7 0.8 copy-start.8
  150.6 9.8 %collective-permute-start.8 = (bf16[256,512]{1,0:T(8,128)(2,1)S(1)}, bf16[256,512]{1,0:T(8,128)(2,1)S(1)}, u32[]{:S(2)}, u32[]{:S(2)}) collective-permute-start(bf16[256,512]{1,0:T(8,128)(2,1)S(1)} %get-tuple-element.45), channel_id=1, source_target_pairs={{0,64},{64,0},{1,65},{65,1},{2,66},{66,2},{3,67},{67,3},{4,68},{68... | collective-permute-start | bytes 786440 | tf_op jit(solution)/shard_map/ppermute | solution.py:230
  154.3 10.6 %collective-permute-start.7 = (bf16[256,512]{1,0:T(8,128)(2,1)S(1)}, bf16[256,512]{1,0:T(8,128)(2,1)S(1)}, u32[]{:S(2)}, u32[]{:S(2)}) collective-permute-start(bf16[256,512]{1,0:T(8,128)(2,1)S(1)} %get-tuple-element.43), channel_id=1, source_target_pairs={{0,64},{64,0},{1,65},{65,1},{2,66},{66,2},{3,67},{67,3},{4,68},{68... | collective-permute-start | bytes 786440 | tf_op jit(solution)/shard_map/ppermute | solution.py:230
  167.2 36.9 %all-to-all-start.2 = ((bf16[16,2,16,2048]{3,2,1,0:T(8,128)(2,1)}), bf16[16,2,16,2048]{3,2,1,0:T(8,128)(2,1)}, u32[]{:S(2)}, u32[]{:S(2)}) async-start(bf16[16,2,16,2048]{3,2,1,0:T(8,128)(2,1)} %get-tuple-element.50), calls=%async_computation.2 | async-start | bytes 4194304 | tf_op jit(solution)/shard_map/all_to_all | solution.py:271
  175.0 2.0 collective-permute-start.9
  175.1 3.5 %collective-permute-start.11 = (bf16[2,256,512]{2,1,0:T(8,128)(2,1)S(1)}, bf16[2,256,512]{2,1,0:T(8,128)(2,1)S(1)}, u32[]{:S(2)}, u32[]{:S(2)}) collective-permute-start(bf16[2,256,512]{2,1,0:T(8,128)(2,1)S(1)} %get-tuple-element.57), channel_id=1, source_target_pairs={{0,8},{8,0},{1,9},{9,1},{2,10},{10,2},{3,11},{11,3},{4,12},{12,4},... | collective-permute-start | bytes 1572872 | tf_op jit(solution)/shard_map/ppermute | solution.py:230
  175.6 3.7 %collective-permute-start.13 = (bf16[2,256,512]{2,1,0:T(8,128)(2,1)S(1)}, bf16[2,256,512]{2,1,0:T(8,128)(2,1)S(1)}, u32[]{:S(2)}, u32[]{:S(2)}) collective-permute-start(bf16[2,256,512]{2,1,0:T(8,128)(2,1)S(1)} %get-tuple-element.59), channel_id=1, source_target_pairs={{0,8},{8,0},{1,9},{9,1},{2,10},{10,2},{3,11},{11,3},{4,12},{12,4},... | collective-permute-start | bytes 1572872 | tf_op jit(solution)/shard_map/ppermute | solution.py:230
  175.7 7.2 %collective-permute-start.15 = (bf16[2,256,512]{2,1,0:T(8,128)(2,1)S(1)}, bf16[2,256,512]{2,1,0:T(8,128)(2,1)S(1)}, u32[]{:S(2)}, u32[]{:S(2)}) collective-permute-start(bf16[2,256,512]{2,1,0:T(8,128)(2,1)S(1)} %get-tuple-element.61), channel_id=1, source_target_pairs={{0,8},{8,0},{1,9},{9,1},{2,10},{10,2},{3,11},{11,3},{4,12},{12,4},... | collective-permute-start | bytes 1572872 | tf_op jit(solution)/shard_map/ppermute | solution.py:230
  177.1 35.6 %collective-permute-start.10 = (bf16[2,256,512]{2,1,0:T(8,128)(2,1)S(1)}, bf16[2,256,512]{2,1,0:T(8,128)(2,1)S(1)}, u32[]{:S(2)}, u32[]{:S(2)}) collective-permute-start(bf16[2,256,512]{2,1,0:T(8,128)(2,1)S(1)} %shard_map.83), channel_id=1, source_target_pairs={{0,32},{16,48},{32,0},{48,16},{1,33},{17,49},{33,1},{49,17},{2,34}... | collective-permute-start | bytes 1572872 | tf_op jit(solution)/shard_map/ppermute | solution.py:226
  178.7 34.0 %collective-permute-start.12 = (bf16[2,256,512]{2,1,0:T(8,128)(2,1)S(1)}, bf16[2,256,512]{2,1,0:T(8,128)(2,1)S(1)}, u32[]{:S(2)}, u32[]{:S(2)}) collective-permute-start(bf16[2,256,512]{2,1,0:T(8,128)(2,1)S(1)} %shard_map.84), channel_id=1, source_target_pairs={{0,16},{16,32},{32,48},{48,0},{1,17},{17,33},{33,49},{49,1},{2,18}... | collective-permute-start | bytes 1572872 | tf_op jit(solution)/shard_map/ppermute | solution.py:226
  180.2 32.4 %collective-permute-start.14 = (bf16[2,256,512]{2,1,0:T(8,128)(2,1)}, bf16[2,256,512]{2,1,0:T(8,128)(2,1)}, u32[]{:S(2)}, u32[]{:S(2)}) collective-permute-start(bf16[2,256,512]{2,1,0:T(8,128)(2,1)} %shard_map.85), channel_id=1, source_target_pairs={{0,48},{16,0},{32,16},{48,32},{1,49},{17,1},{33,17},{49,33},{2,50}... | collective-permute-start | bytes 1572872 | tf_op jit(solution)/shard_map/ppermute | solution.py:226

commit v2 on v1

--- a/solution.py
+++ b/solution.py
@@ -112,10 +112,11 @@
         for t in range(2):
             block = a_ref[:, 2 * t : 2 * t + 2, :, cols].reshape(ROWS, 512)
             mixed = jnp.dot(mixing_t, block, preferred_element_type=F32)
-            held[half, :, t, :, part] = mixed.astype(BF).reshape(EXPERTS, POS, 512)
-        place = (half, slice(None), slice(None), slice(None), part)
-        copies.append(pltpu.make_async_copy(held.at[place], f_ref.at[place], sem.at[j]))
-        copies[j].start()
+            held[:, half, t, :, part] = mixed.astype(BF).reshape(EXPERTS, POS, 512)
+        if j % 4 == 3:
+            place = (slice(None), half)
+            copies.append(pltpu.make_async_copy(held.at[place], f_ref.at[place], sem.at[j]))
+            copies[-1].start()
     for copy in copies:
         copy.wait()
 
@@ -178,13 +179,13 @@
                 out_refs[2 * n + j][t] = tn(block, ref[...]).astype(BF)
 
 
-def add_kernel(keep_ref, got_ref, o_ref):
-    o_ref[...] = (keep_ref[...].astype(F32) + got_ref[...].astype(F32)).astype(o_ref.dtype)
-
-
-def sum_kernel(own_ref, a_ref, b_ref, c_ref, in_ref, out_ref):
-    for t, ref in enumerate((in_ref, out_ref)):
-        ref[0] = own_ref[t] + a_ref[t].astype(F32) + b_ref[t].astype(F32) + c_ref[t].astype(F32)
+def add_kernel(keep_ref, got_ref, *o_refs):
+    for t, o_ref in enumerate(o_refs):
+        o_ref[...] = (keep_ref[t].astype(F32) + got_ref[t].astype(F32)).astype(o_ref.dtype)
+
+
+def sum_kernel(own_ref, a_ref, b_ref, c_ref, o_ref):
+    o_ref[0] = own_ref[...] + a_ref[...].astype(F32) + b_ref[...].astype(F32) + c_ref[...].astype(F32)
 
 
 def final_kernel(b_ref, probs_ref, mixing_ref, rows_ref, far_rxt_ref, o_ref, a_ref, rxt_ref, held, in_sem, sem):
@@ -199,10 +200,10 @@
     for j in range(8):
         cols = pl.ds(j * 512, 512)
         reads[j].wait()
-        half, part = pl.ds(j // 4 * EXPERTS, EXPERTS), pl.ds(j % 4 * 512, 512)
+        half, part = j // 4, pl.ds(j % 4 * 512, 512)
         for t in range(2):
             block = a_ref[:, 2 - 2 * t : 4 - 2 * t, :, cols].reshape(ROWS, 512)
-            weight_grad += nt(b_ref[half, t, :, part].reshape(LANES, 512), block)
+            weight_grad += nt(b_ref[:, half, t, :, part].reshape(LANES, 512), block)
     probs = probs_ref[...].reshape(SEQS, POS, LANES)
     weight_grad = weight_grad.T.reshape(SEQS, POS, LANES)
     mean = jnp.sum(probs * weight_grad, axis=0, keepdims=True)
@@ -212,8 +213,8 @@
     copies = []
     for j in range(8):
         cols = pl.ds(j * 512, 512)
-        half, part = pl.ds(j // 4 * EXPERTS, EXPERTS), pl.ds(j % 4 * 512, 512)
-        right = jnp.concatenate([b_ref[half, 1, :, part].reshape(LANES, 512), rxt_ref[:, cols]], axis=0)
+        half, part = j // 4, pl.ds(j % 4 * 512, 512)
+        right = jnp.concatenate([b_ref[:, half, 1, :, part].reshape(LANES, 512), rxt_ref[:, cols]], axis=0)
         out = jnp.dot(both, right, preferred_element_type=F32)
         held[:, :, cols] = out.astype(BF).reshape(SEQS, POS, 512)
         copies.append(pltpu.make_async_copy(held.at[:, :, cols], o_ref.at[:, :, cols], sem.at[j]))
@@ -235,12 +236,12 @@
     rows = lax.all_to_all(rows, ("yh", "x", "c"), 0, 0, tiled=True)
     mixed, probs, mixing = call(
         mix_kernel,
-        (pltpu.HBM((2, EXPERTS, 2, POS, HALF), BF), shape((ROWS, LANES), F32), shape((ROWS, LANES), BF)),
+        (pltpu.HBM((EXPERTS, 2, 2, POS, HALF), BF), shape((ROWS, LANES), F32), shape((ROWS, LANES), BF)),
         2, 3 * 10**9, 12 * MIB, 22, specs=(HBM, VM, VM),
-        scratch=[pltpu.VMEM((2, EXPERTS, 2, POS, HALF), BF), pltpu.SemaphoreType.DMA((8,))],
+        scratch=[pltpu.VMEM((EXPERTS, 2, 2, POS, HALF), BF), pltpu.SemaphoreType.DMA((8,))],
     )(rows, rxt)
 
-    experts = ("yh", "z", "yl")
+    experts = ("z", "yl", "yh")
     got = lax.all_to_all(mixed.reshape(16, 2, POS, HALF), experts, 0, 0, tiled=True)
 
     shard, _ = lax.optimization_barrier((shard, mixing))
@@ -275,9 +276,17 @@
     sums = []
     for n, k in enumerate(ORDER):
         got_part = swap(parts[2 * n + 1], "c")
-        total = shape((2, SHARD, HID), BF if k else F32)
-        sums.append(call(add_kernel, total, 2, 10**6, 2 * MIB, 4)(parts[2 * n], got_part))
-    sums = [shift(x, k) if k else x for x, k in zip(sums, ORDER)]
+        total = shape((SHARD, HID), BF if k else F32)
+        sums.append(call(add_kernel, (total, total), 2, 10**6, 2 * MIB, 4)(parts[2 * n], got_part))
+
+    def group_sum(t, after):
+        terms = lax.optimization_barrier(tuple(x[t] for x in sums) + after)[:4]
+        terms = [shift(x, k) if k else x for x, k in zip(terms, ORDER)]
+        return terms, call(sum_kernel, shape((1, SHARD, HID), F32), 4, 10**6, 4 * MIB, 4)
+
+    terms, add_up = group_sum(1, ())
+    grad_out = add_up(terms[3], *terms[:3])
+    terms, add_up = group_sum(0, ())
     token_grad = call(
         final_kernel, shape((SEQS, POS, D), BF), 3, 4 * 10**9, 16 * MIB, 32, specs=HBM, far=2,
         scratch=[
@@ -287,12 +296,9 @@
             pltpu.SemaphoreType.DMA((9,)),
             pltpu.SemaphoreType.DMA((8,)),
         ],
-    )(back, probs, mixing, in_hbm(rows), in_hbm(rxt))
-    token_grad, *sums = lax.optimization_barrier((token_grad, *sums))
-    grad = shape((1, SHARD, HID), F32)
-    grad_in, grad_out = call(sum_kernel, (grad, grad), 4, 10**6, 4 * MIB, 6)(
-        sums[3], sums[0], sums[1], sums[2]
-    )
+    )(back.reshape(EXPERTS, 2, 2, POS, HALF), probs, mixing, in_hbm(rows), in_hbm(rxt))
+    token_grad, *terms = lax.optimization_barrier((token_grad, *terms))
+    grad_in = add_up(terms[3], *terms[:3])
     return token_grad, grad_in, grad_out
 
 

time: 215 us -> 211 us (0.981)
  waiting for transfers between devices: 56.5 us -> 50.4 us
  starting transfers between devices: 23.8 us -> 26.2 us
    all_to_all x1, waiting for transfers between devices: 21.1 us -> 3.89 us  [on_device(): back = lax.all_to_all(back, experts, 0, 0, tiled=True)]
    ppermute x6 -> x9, waiting for transfers between devices: 24.7 us -> 34.5 us  [shift(): return lax.ppermute(x, 'x', [(i, (i + k) % 4) for i in range(4)])]
    ppermute x10, waiting for transfers between devices: 8.69 us -> 12 us  [swap(): return lax.ppermute(x, axis, [(0, 1), (1, 0)])]
    ppermute x6 -> x9, starting transfers between devices: 7.01 us -> 8.96 us  [shift(): return lax.ppermute(x, 'x', [(i, (i + k) % 4) for i in range(4)])]
    pallas_call x6 -> x7, Pallas kernels: 7.45 us -> 6.38 us  [the longest x1 4.11 us: on_device(): call(mix_kernel, (pltpu.HBM((EXPERTS, 2, 2, POS, HALF), BF), shape((ROWS,...]
  transfers between devices with their start and end apart: 18 -> 21, of which waited for: 9 -> 13; matrix products, arithmetic and copies ran while one was open for 0% -> 0% of each run, Pallas kernels for 6% -> 7%
where the time goes in v2:
time: 211 us; the launch traced here: 210 us
  blocking collectives  104 us (49%)
  waiting for transfers between devices  50.4 us (24%)
  Pallas kernels  27.1 us (13%)
  starting transfers between devices  26.2 us (12%)
    all_to_all x1, blocking collectives, on_device(): rows = lax.all_to_all(rows, ('yh', 'x', 'c'), 0, 0, tiled=True)  104 us
    ppermute x9, waiting for transfers between devices, shift(): return lax.ppermute(x, 'x', [(i, (i + k) % 4) for i in range(4)])  34.5 us
    ppermute x10, waiting for transfers between devices, swap(): return lax.ppermute(x, axis, [(0, 1), (1, 0)])  12 us
    ppermute x9, starting transfers between devices, shift(): return lax.ppermute(x, 'x', [(i, (i + k) % 4) for i in range(4)])  8.96 us
    pallas_call x1, Pallas kernels, on_device(): call(final_kernel, shape((SEQS, POS, D), BF), 3, 4 * 10 ** 9, 16 * MIB, 3...  8.49 us
    all_to_all x1, starting transfers between devices, on_device(): back = lax.all_to_all(back, experts, 0, 0, tiled=True)  6.93 us
    all_to_all x1, starting transfers between devices, on_device(): lax.all_to_all(mixed.reshape(16, 2, POS, HALF), experts, 0, 0, tiled=True)  5.54 us
    ppermute x10, starting transfers between devices, swap(): return lax.ppermute(x, axis, [(0, 1), (1, 0)])  4.8 us
  transfers between devices with their start and end apart: 21, of which 13 were waited for; matrix products, arithmetic and copies ran while one was open for 0% of the time, Pallas kernels for 7%

profile of v2, /device:TPU:0, one launch (start us, length us, event | category | flops | bytes accessed | tf_op | source)
XLA Modules:
  0.0 210.1 jit_solution(15660801296076240888)
XLA Ops:
  0.6 3.7 %pack.1 = (bf16[16,4,16,4096]{3,2,1,0:T(8,128)(2,1)S(1)}, bf16[2,256,512]{2,1,0:T(8,128)(2,1)S(1)}, bf16[128,4096]{1,0:T(8,128)(2,1)S(1)}) custom-call(bf16[2,16,16,4096]{3,2,1,0:T(8,128)(2,1)} %bitcast.5, bf16[2,16,16,4096]{3,2,1,0:T(8,128)(2,1)} %bitcast.6, bf16[1,256,512]{2,1,0:T(8,128)(2,1)} %wi_ref.1, bf16[1,256,512]{2,1,0:T(8,128)(2,1)} %wo_ref.1, ...), custom_call_target="tpu_custom_call" | custom-call | flops 8388608 | bytes 16777216 | tf_op jit(solution)/shard_map/pack/pallas_call | solution.py:78
  4.4 103.5 %all_to_all.15.a_ref.rows_ref = bf16[16,4,16,4096]{3,2,1,0:T(8,128)(2,1)S(1)} all-to-all(bf16[16,4,16,4096]{3,2,1,0:T(8,128)(2,1)S(1)} %get-tuple-element.50), channel_id=1, replica_groups=mesh['yh'=2,'x'=4,'c'=2,'z'=4,'yl'=2] {'yh','x','c'}, dimensions={0} | all-to-all | bytes 16777216 | tf_op jit(solution)/shard_map/all_to_all | solution.py:236
  107.9 4.1 %shard_map.76 = (bf16[8,2,2,16,2048]{4,3,2,1,0:T(8,128)(2,1)}, f32[512,128]{1,0:T(8,128)S(1)}, bf16[512,128]{1,0:T(8,128)(2,1)S(1)}) custom-call(bf16[16,4,16,4096]{3,2,1,0:T(8,128)(2,1)S(1)} %all_to_all.15.a_ref.rows_ref, bf16[128,4096]{1,0:T(8,128)(2,1)S(1)} %get-tuple-element.51.rxt_ref.far_rxt_ref), custom_call_target="tpu_custom_call" | custom-call | flops 3000000000 | bytes 12582912 | tf_op jit(solution)/shard_map/pallas_call | solution.py:237
  112.0 5.5 %all-to-all-start.1 = ((bf16[16,2,16,2048]{3,2,1,0:T(8,128)(2,1)}), bf16[16,2,16,2048]{3,2,1,0:T(8,128)(2,1)S(1)}, u32[]{:S(2)}, u32[]{:S(2)}) async-start(bf16[16,2,16,2048]{3,2,1,0:T(8,128)(2,1)} %bitcast.7), calls=%async_computation.1 | async-start | bytes 4194304 | tf_op jit(solution)/shard_map/all_to_all | solution.py:245
  117.6 0.8 collective-permute-start.5
  118.4 0.8 collective-permute-start.3
  119.2 0.7 collective-permute-start.1
  119.9 12.6 %collective-permute-done.5.refs_6_ = bf16[2,256,512]{2,1,0:T(8,128)(2,1)S(1)} collective-permute-done((bf16[2,256,512]{2,1,0:T(8,128)(2,1)S(1)}, bf16[2,256,512]{2,1,0:T(8,128)(2,1)S(1)}, u32[]{:S(2)}, u32[]{:S(2)}) %collective-permute-start.5) | collective-permute-done | bytes 524320 | tf_op jit(solution)/shard_map/ppermute | solution.py:227
  132.5 2.3 %collective-permute-done.3.refs_4_ = bf16[2,256,512]{2,1,0:T(8,128)(2,1)S(1)} collective-permute-done((bf16[2,256,512]{2,1,0:T(8,128)(2,1)S(1)}, bf16[2,256,512]{2,1,0:T(8,128)(2,1)S(1)}, u32[]{:S(2)}, u32[]{:S(2)}) %collective-permute-start.3) | collective-permute-done | bytes 524320 | tf_op jit(solution)/shard_map/ppermute | solution.py:227
  134.8 9.8 %collective-permute-done.1.refs_2_ = bf16[2,256,512]{2,1,0:T(8,128)(2,1)S(1)} collective-permute-done((bf16[2,256,512]{2,1,0:T(8,128)(2,1)S(1)}, bf16[2,256,512]{2,1,0:T(8,128)(2,1)S(1)}, u32[]{:S(2)}, u32[]{:S(2)}) %collective-permute-start.1) | collective-permute-done | bytes 524320 | tf_op jit(solution)/shard_map/ppermute | solution.py:227
  144.7 0.8 copy-done.5
  145.8 0.8 copy-done.8
  146.7 2.1 shard_map.78
  148.7 3.2 %collective-permute-start.8 = (bf16[256,512]{1,0:T(8,128)(2,1)S(1)}, bf16[256,512]{1,0:T(8,128)(2,1)S(1)}, u32[]{:S(2)}, u32[]{:S(2)}) collective-permute-start(bf16[256,512]{1,0:T(8,128)(2,1)S(1)} %get-tuple-element.59), channel_id=1, source_target_pairs={{0,64},{64,0},{1,65},{65,1},{2,66},{66,2},{3,67},{67,3},{4,68},{68... | collective-permute-start | bytes 786440 | tf_op jit(solution)/shard_map/ppermute | solution.py:231
  151.9 2.1 shard_map.77
  154.5 5.0 %collective-permute-done.8.other_ref = bf16[256,512]{1,0:T(8,128)(2,1)S(1)} collective-permute-done((bf16[256,512]{1,0:T(8,128)(2,1)S(1)}, bf16[256,512]{1,0:T(8,128)(2,1)S(1)}, u32[]{:S(2)}, u32[]{:S(2)}) %collective-permute-start.8) | collective-permute-done | bytes 262176 | tf_op jit(solution)/shard_map/ppermute | solution.py:231
  159.5 0.8 shard_map.79
  160.2 4.2 %collective-permute-done.7.other_ref = bf16[256,512]{1,0:T(8,128)(2,1)S(1)} collective-permute-done((bf16[256,512]{1,0:T(8,128)(2,1)S(1)}, bf16[256,512]{1,0:T(8,128)(2,1)S(1)}, u32[]{:S(2)}, u32[]{:S(2)}) %collective-permute-start.7) | collective-permute-done | bytes 262176 | tf_op jit(solution)/shard_map/ppermute | solution.py:231
  164.4 2.3 %shard_map.80 = (bf16[16,2,16,2048]{3,2,1,0:T(8,128)(2,1)}, bf16[256,512]{1,0:T(8,128)(2,1)S(1)}) custom-call(f32[256,512]{1,0:T(8,128)S(1)} %get-tuple-element.56.own_ref, bf16[256,512]{1,0:T(8,128)(2,1)S(1)} %collective-permute-done.7.other_ref, f32[256,512]{1,0:T(8,128)S(1)} %get-tuple-element.61.pre_ref, ...), custom_call_target="tpu_custom_call" | custom-call | flops 1000000000 | bytes 4194304 | tf_op jit(solution)/shard_map/pallas_call | solution.py:267
  166.8 6.9 %all-to-all-start.2 = ((bf16[16,2,16,2048]{3,2,1,0:T(8,128)(2,1)}), bf16[16,2,16,2048]{3,2,1,0:T(8,128)(2,1)}, u32[]{:S(2)}, u32[]{:S(2)}) async-start(bf16[16,2,16,2048]{3,2,1,0:T(8,128)(2,1)} %get-tuple-element.64), calls=%async_computation.2 | async-start | bytes 4194304 | tf_op jit(solution)/shard_map/all_to_all | solution.py:272
  173.7 1.3 shard_map.82
  176.1 0.9 collective-permute-done.9.got_ref
  179.4 1.4 collective-permute-start.16
  181.4 2.7 %collective-permute-start.18 = (bf16[256,512]{1,0:T(8,128)(2,1)S(1)}, bf16[256,512]{1,0:T(8,128)(2,1)S(1)}, u32[]{:S(2)}, u32[]{:S(2)}) collective-permute-start(bf16[256,512]{1,0:T(8,128)(2,1)S(1)} %get-tuple-element.96), channel_id=1, source_target_pairs={{0,48},{16,0},{32,16},{48,32},{1,49},{17,1},{33,17},{49,33},{2,50}... | collective-permute-start | bytes 786440 | tf_op jit(solution)/shard_map/ppermute | solution.py:227
  184.0 1.0 collective-permute-start.13
  185.0 5.2 %collective-permute-done.16.a_ref = bf16[256,512]{1,0:T(8,128)(2,1)S(1)} collective-permute-done((bf16[256,512]{1,0:T(8,128)(2,1)S(1)}, bf16[256,512]{1,0:T(8,128)(2,1)S(1)}, u32[]{:S(2)}, u32[]{:S(2)}) %collective-permute-start.16) | collective-permute-done | bytes 262176 | tf_op jit(solution)/shard_map/ppermute | solution.py:227
  190.2 1.1 collective-permute-start.15
  191.2 4.6 %collective-permute-done.17.b_ref = bf16[256,512]{1,0:T(8,128)(2,1)S(1)} collective-permute-done((bf16[256,512]{1,0:T(8,128)(2,1)S(1)}, bf16[256,512]{1,0:T(8,128)(2,1)S(1)}, u32[]{:S(2)}, u32[]{:S(2)}) %collective-permute-start.17) | collective-permute-done | bytes 262176 | tf_op jit(solution)/shard_map/ppermute | solution.py:227
  195.9 0.9 shard_map.88
  196.8 3.9 %all-to-all-done.2 = bf16[16,2,16,2048]{3,2,1,0:T(8,128)(2,1)} async-done(((bf16[16,2,16,2048]{3,2,1,0:T(8,128)(2,1)}), bf16[16,2,16,2048]{3,2,1,0:T(8,128)(2,1)}, u32[]{:S(2)}, u32[]{:S(2)}) %all-to-all-start.2) | async-done | bytes 2097184 | tf_op jit(solution)/shard_map/all_to_all | solution.py:272
  200.7 8.5 %shard_map.81 = bf16[32,16,4096]{2,1,0:T(8,128)(2,1)} custom-call(bf16[8,2,2,16,2048]{4,3,2,1,0:T(8,128)(2,1)} %bitcast.4.b_ref, f32[512,128]{1,0:T(8,128)S(1)} %get-tuple-element.65.probs_ref, bf16[512,128]{1,0:T(8,128)(2,1)S(1)} %get-tuple-element.54.mixing_ref, bf16[16,4,16,4096]{3,2,1,0:T(8,128)(2,1)} %copy-done, bf16[128,4096]{1,0:T(8,128)(2,1)} %copy-done.2), custom_call_target="tpu_custom_call" | custom-call | flops 4000000000 | bytes 16777216 | tf_op jit(solution)/shard_map/pallas_call | solution.py:290
  209.2 0.9 shard_map.87
  (43 shorter events, 5.0 us)
Async XLA Ops:
  4.3 103.6 %copy-start.2 = (bf16[128,4096]{1,0:T(8,128)(2,1)}, bf16[128,4096]{1,0:T(8,128)(2,1)S(1)}, u32[]{:S(2)}) copy-start(bf16[128,4096]{1,0:T(8,128)(2,1)S(1)} %get-tuple-element.51.rxt_ref.far_rxt_ref) | copy-start | bytes 3145732
  4.4 115.5 %copy-start.1 = (bf16[2,256,512]{2,1,0:T(8,128)(2,1)}, bf16[2,256,512]{2,1,0:T(8,128)(2,1)S(1)}, u32[]{:S(2)}) copy-start(bf16[2,256,512]{2,1,0:T(8,128)(2,1)S(1)} %get-tuple-element.55.refs_0_) | copy-start | bytes 1572868
  107.9 4.1 %copy-start = (bf16[16,4,16,4096]{3,2,1,0:T(8,128)(2,1)}, bf16[16,4,16,4096]{3,2,1,0:T(8,128)(2,1)S(1)}, u32[]{:S(2)}) copy-start(bf16[16,4,16,4096]{3,2,1,0:T(8,128)(2,1)S(1)} %all_to_all.15.a_ref.rows_ref) | copy-start | bytes 25165828
  112.0 34.6 %all-to-all-start.1 = ((bf16[16,2,16,2048]{3,2,1,0:T(8,128)(2,1)}), bf16[16,2,16,2048]{3,2,1,0:T(8,128)(2,1)S(1)}, u32[]{:S(2)}, u32[]{:S(2)}) async-start(bf16[16,2,16,2048]{3,2,1,0:T(8,128)(2,1)} %bitcast.7), calls=%async_computation.1 | async-start | bytes 4194304 | tf_op jit(solution)/shard_map/all_to_all | solution.py:245
  117.6 14.9 %collective-permute-start.5 = (bf16[2,256,512]{2,1,0:T(8,128)(2,1)S(1)}, bf16[2,256,512]{2,1,0:T(8,128)(2,1)S(1)}, u32[]{:S(2)}, u32[]{:S(2)}) collective-permute-start(bf16[2,256,512]{2,1,0:T(8,128)(2,1)S(1)} %get-tuple-element.55.refs_0_), channel_id=1, source_target_pairs={{0,48},{16,0},{32,16},{48,32},{1,49},{17,1},{33,17},{49,33},{2,50}... | collective-permute-start | bytes 1572872 | tf_op jit(solution)/shard_map/ppermute | solution.py:227
  118.4 16.3 %collective-permute-start.3 = (bf16[2,256,512]{2,1,0:T(8,128)(2,1)S(1)}, bf16[2,256,512]{2,1,0:T(8,128)(2,1)S(1)}, u32[]{:S(2)}, u32[]{:S(2)}) collective-permute-start(bf16[2,256,512]{2,1,0:T(8,128)(2,1)S(1)} %get-tuple-element.55.refs_0_), channel_id=1, source_target_pairs={{0,32},{16,48},{32,0},{48,16},{1,33},{17,49},{33,1},{49,17},{2,34}... | collective-permute-start | bytes 1572872 | tf_op jit(solution)/shard_map/ppermute | solution.py:227
  119.2 25.4 %collective-permute-start.1 = (bf16[2,256,512]{2,1,0:T(8,128)(2,1)S(1)}, bf16[2,256,512]{2,1,0:T(8,128)(2,1)S(1)}, u32[]{:S(2)}, u32[]{:S(2)}) collective-permute-start(bf16[2,256,512]{2,1,0:T(8,128)(2,1)S(1)} %get-tuple-element.55.refs_0_), channel_id=1, source_target_pairs={{0,16},{16,32},{32,48},{48,0},{1,17},{17,33},{33,49},{49,1},{2,18}... | collective-permute-start | bytes 1572872 | tf_op jit(solution)/shard_map/ppermute | solution.py:227
  119.9 24.8 %collective-permute-start = (bf16[2,256,512]{2,1,0:T(8,128)(2,1)S(1)}, bf16[2,256,512]{2,1,0:T(8,128)(2,1)S(1)}, u32[]{:S(2)}, u32[]{:S(2)}) collective-permute-start(bf16[2,256,512]{2,1,0:T(8,128)(2,1)S(1)} %get-tuple-element.55.refs_0_), channel_id=1, source_target_pairs={{0,8},{8,0},{1,9},{9,1},{2,10},{10,2},{3,11},{11,3},{4,12},{12,4},... | collective-permute-start | bytes 1572872 | tf_op jit(solution)/shard_map/ppermute | solution.py:231
  132.5 14.2 %copy-start.3 = (bf16[2,256,512]{2,1,0:T(8,128)(2,1)}, bf16[2,256,512]{2,1,0:T(8,128)(2,1)S(1)}, u32[]{:S(2)}) copy-start(bf16[2,256,512]{2,1,0:T(8,128)(2,1)S(1)} %collective-permute-done.5.refs_6_) | copy-start | bytes 1572868
  132.5 12.2 %collective-permute-start.6 = (bf16[2,256,512]{2,1,0:T(8,128)(2,1)S(1)}, bf16[2,256,512]{2,1,0:T(8,128)(2,1)S(1)}, u32[]{:S(2)}, u32[]{:S(2)}) collective-permute-start(bf16[2,256,512]{2,1,0:T(8,128)(2,1)S(1)} %collective-permute-done.5.refs_6_), channel_id=1, source_target_pairs={{0,8},{8,0},{1,9},{9,1},{2,10},{10,2},{3,11},{11,3},{4,12},{12,4},... | collective-permute-start | bytes 1572872 | tf_op jit(solution)/shard_map/ppermute | solution.py:231
  134.7 9.9 %copy-start.4 = (bf16[2,256,512]{2,1,0:T(8,128)(2,1)}, bf16[2,256,512]{2,1,0:T(8,128)(2,1)S(1)}, u32[]{:S(2)}) copy-start(bf16[2,256,512]{2,1,0:T(8,128)(2,1)S(1)} %collective-permute-done.3.refs_4_) | copy-start | bytes 1572868
  134.7 9.9 %collective-permute-start.4 = (bf16[2,256,512]{2,1,0:T(8,128)(2,1)S(1)}, bf16[2,256,512]{2,1,0:T(8,128)(2,1)S(1)}, u32[]{:S(2)}, u32[]{:S(2)}) collective-permute-start(bf16[2,256,512]{2,1,0:T(8,128)(2,1)S(1)} %collective-permute-done.3.refs_4_), channel_id=1, source_target_pairs={{0,8},{8,0},{1,9},{9,1},{2,10},{10,2},{3,11},{11,3},{4,12},{12,4},... | collective-permute-start | bytes 1572872 | tf_op jit(solution)/shard_map/ppermute | solution.py:231
  144.6 0.8 copy-start.5
  144.6 2.0 collective-permute-start.2
  144.6 0.9 copy-start.6
  144.6 1.1 copy-start.7
  145.8 0.8 copy-start.8
  148.7 10.7 %collective-permute-start.8 = (bf16[256,512]{1,0:T(8,128)(2,1)S(1)}, bf16[256,512]{1,0:T(8,128)(2,1)S(1)}, u32[]{:S(2)}, u32[]{:S(2)}) collective-permute-start(bf16[256,512]{1,0:T(8,128)(2,1)S(1)} %get-tuple-element.59), channel_id=1, source_target_pairs={{0,64},{64,0},{1,65},{65,1},{2,66},{66,2},{3,67},{67,3},{4,68},{68... | collective-permute-start | bytes 786440 | tf_op jit(solution)/shard_map/ppermute | solution.py:231
  154.0 10.5 %collective-permute-start.7 = (bf16[256,512]{1,0:T(8,128)(2,1)S(1)}, bf16[256,512]{1,0:T(8,128)(2,1)S(1)}, u32[]{:S(2)}, u32[]{:S(2)}) collective-permute-start(bf16[256,512]{1,0:T(8,128)(2,1)S(1)} %get-tuple-element.57), channel_id=1, source_target_pairs={{0,64},{64,0},{1,65},{65,1},{2,66},{66,2},{3,67},{67,3},{4,68},{68... | collective-permute-start | bytes 786440 | tf_op jit(solution)/shard_map/ppermute | solution.py:231
  166.8 33.9 %all-to-all-start.2 = ((bf16[16,2,16,2048]{3,2,1,0:T(8,128)(2,1)}), bf16[16,2,16,2048]{3,2,1,0:T(8,128)(2,1)}, u32[]{:S(2)}, u32[]{:S(2)}) async-start(bf16[16,2,16,2048]{3,2,1,0:T(8,128)(2,1)} %get-tuple-element.64), calls=%async_computation.2 | async-start | bytes 4194304 | tf_op jit(solution)/shard_map/all_to_all | solution.py:272
  175.0 2.0 collective-permute-start.9
  175.1 2.6 %collective-permute-start.10 = (bf16[2,256,512]{2,1,0:T(8,128)(2,1)S(1)}, bf16[2,256,512]{2,1,0:T(8,128)(2,1)S(1)}, u32[]{:S(2)}, u32[]{:S(2)}) collective-permute-start(bf16[2,256,512]{2,1,0:T(8,128)(2,1)S(1)} %get-tuple-element.72), channel_id=1, source_target_pairs={{0,8},{8,0},{1,9},{9,1},{2,10},{10,2},{3,11},{11,3},{4,12},{12,4},... | collective-permute-start | bytes 1572872 | tf_op jit(solution)/shard_map/ppermute | solution.py:231
  175.6 2.9 %collective-permute-start.11 = (bf16[2,256,512]{2,1,0:T(8,128)(2,1)S(1)}, bf16[2,256,512]{2,1,0:T(8,128)(2,1)S(1)}, u32[]{:S(2)}, u32[]{:S(2)}) collective-permute-start(bf16[2,256,512]{2,1,0:T(8,128)(2,1)S(1)} %get-tuple-element.75), channel_id=1, source_target_pairs={{0,8},{8,0},{1,9},{9,1},{2,10},{10,2},{3,11},{11,3},{4,12},{12,4},... | collective-permute-start | bytes 1572872 | tf_op jit(solution)/shard_map/ppermute | solution.py:231
  175.7 3.6 %collective-permute-start.12 = (bf16[2,256,512]{2,1,0:T(8,128)(2,1)S(1)}, bf16[2,256,512]{2,1,0:T(8,128)(2,1)S(1)}, u32[]{:S(2)}, u32[]{:S(2)}) collective-permute-start(bf16[2,256,512]{2,1,0:T(8,128)(2,1)S(1)} %get-tuple-element.78), channel_id=1, source_target_pairs={{0,8},{8,0},{1,9},{9,1},{2,10},{10,2},{3,11},{11,3},{4,12},{12,4},... | collective-permute-start | bytes 1572872 | tf_op jit(solution)/shard_map/ppermute | solution.py:231
  179.4 10.8 %collective-permute-start.16 = (bf16[256,512]{1,0:T(8,128)(2,1)S(1)}, bf16[256,512]{1,0:T(8,128)(2,1)S(1)}, u32[]{:S(2)}, u32[]{:S(2)}) collective-permute-start(bf16[256,512]{1,0:T(8,128)(2,1)S(1)} %get-tuple-element.94), channel_id=1, source_target_pairs={{0,32},{16,48},{32,0},{48,16},{1,33},{17,49},{33,1},{49,17},{2,34}... | collective-permute-start | bytes 786440 | tf_op jit(solution)/shard_map/ppermute | solution.py:227
  180.8 15.1 %collective-permute-start.17 = (bf16[256,512]{1,0:T(8,128)(2,1)S(1)}, bf16[256,512]{1,0:T(8,128)(2,1)S(1)}, u32[]{:S(2)}, u32[]{:S(2)}) collective-permute-start(bf16[256,512]{1,0:T(8,128)(2,1)S(1)} %get-tuple-element.95), channel_id=1, source_target_pairs={{0,16},{16,32},{32,48},{48,0},{1,17},{17,33},{33,49},{49,1},{2,18}... | collective-permute-start | bytes 786440 | tf_op jit(solution)/shard_map/ppermute | solution.py:227
  181.4 14.5 %collective-permute-start.18 = (bf16[256,512]{1,0:T(8,128)(2,1)S(1)}, bf16[256,512]{1,0:T(8,128)(2,1)S(1)}, u32[]{:S(2)}, u32[]{:S(2)}) collective-permute-start(bf16[256,512]{1,0:T(8,128)(2,1)S(1)} %get-tuple-element.96), channel_id=1, source_target_pairs={{0,48},{16,0},{32,16},{48,32},{1,49},{17,1},{33,17},{49,33},{2,50}... | collective-permute-start | bytes 786440 | tf_op jit(solution)/shard_map/ppermute | solution.py:227
  184.0 25.1 %collective-permute-start.13 = (bf16[256,512]{1,0:T(8,128)(2,1)S(1)}, bf16[256,512]{1,0:T(8,128)(2,1)S(1)}, u32[]{:S(2)}, u32[]{:S(2)}) collective-permute-start(bf16[256,512]{1,0:T(8,128)(2,1)S(1)} %get-tuple-element.80), channel_id=1, source_target_pairs={{0,32},{16,48},{32,0},{48,16},{1,33},{17,49},{33,1},{49,17},{2,34}... | collective-permute-start | bytes 786440 | tf_op jit(solution)/shard_map/ppermute | solution.py:227
  185.0 24.2 %collective-permute-start.14 = (bf16[256,512]{1,0:T(8,128)(2,1)S(1)}, bf16[256,512]{1,0:T(8,128)(2,1)S(1)}, u32[]{:S(2)}, u32[]{:S(2)}) collective-permute-start(bf16[256,512]{1,0:T(8,128)(2,1)S(1)} %get-tuple-element.81), channel_id=1, source_target_pairs={{0,16},{16,32},{32,48},{48,0},{1,17},{17,33},{33,49},{49,1},{2,18}... | collective-permute-start | bytes 786440 | tf_op jit(solution)/shard_map/ppermute | solution.py:227
  190.2 19.0 %collective-permute-start.15 = (bf16[256,512]{1,0:T(8,128)(2,1)S(1)}, bf16[256,512]{1,0:T(8,128)(2,1)S(1)}, u32[]{:S(2)}, u32[]{:S(2)}) collective-permute-start(bf16[256,512]{1,0:T(8,128)(2,1)S(1)} %get-tuple-element.82), channel_id=1, source_target_pairs={{0,48},{16,0},{32,16},{48,32},{1,49},{17,1},{33,17},{49,33},{2,50}... | collective-permute-start | bytes 786440 | tf_op jit(solution)/shard_map/ppermute | solution.py:227

commit v3 on v2

--- a/solution.py
+++ b/solution.py
@@ -113,8 +113,9 @@
             block = a_ref[:, 2 * t : 2 * t + 2, :, cols].reshape(ROWS, 512)
             mixed = jnp.dot(mixing_t, block, preferred_element_type=F32)
             held[:, half, t, :, part] = mixed.astype(BF).reshape(EXPERTS, POS, 512)
-        if j % 4 == 3:
-            place = (slice(None), half)
+        if j in (3, 5, 7):
+            first = max(j - 5, 0) * 512
+            place = (slice(None), half, slice(None), slice(None), pl.ds(first, HALF if j == 3 else 1024))
             copies.append(pltpu.make_async_copy(held.at[place], f_ref.at[place], sem.at[j]))
             copies[-1].start()
     for copy in copies:

time: 211 us -> 211 us (level)
  no operation moved by 1% of the time
where the time goes in v3:
time: 211 us; the launch traced here: 210 us
  blocking collectives  104 us (49%)
  waiting for transfers between devices  50.4 us (24%)
  Pallas kernels  27.1 us (13%)
  starting transfers between devices  26.3 us (12%)
    all_to_all x1, blocking collectives, on_device(): rows = lax.all_to_all(rows, ('yh', 'x', 'c'), 0, 0, tiled=True)  104 us
    ppermute x9, waiting for transfers between devices, shift(): return lax.ppermute(x, 'x', [(i, (i + k) % 4) for i in range(4)])  34.5 us
    ppermute x10, waiting for transfers between devices, swap(): return lax.ppermute(x, axis, [(0, 1), (1, 0)])  12 us
    ppermute x9, starting transfers between devices, shift(): return lax.ppermute(x, 'x', [(i, (i + k) % 4) for i in range(4)])  8.97 us
    pallas_call x1, Pallas kernels, on_device(): call(final_kernel, shape((SEQS, POS, D), BF), 3, 4 * 10 ** 9, 16 * MIB, 3...  8.49 us
    all_to_all x1, starting transfers between devices, on_device(): back = lax.all_to_all(back, experts, 0, 0, tiled=True)  6.94 us
    all_to_all x1, starting transfers between devices, on_device(): lax.all_to_all(mixed.reshape(16, 2, POS, HALF), experts, 0, 0, tiled=True)  5.54 us
    ppermute x10, starting transfers between devices, swap(): return lax.ppermute(x, axis, [(0, 1), (1, 0)])  4.8 us
  transfers between devices with their start and end apart: 21, of which 13 were waited for; matrix products, arithmetic and copies ran while one was open for 0% of the time, Pallas kernels for 7%

profile of v3, /device:TPU:0, one launch (start us, length us, event | category | flops | bytes accessed | tf_op | source)
XLA Modules:
  0.0 210.1 jit_solution(11476053179858156798)
XLA Ops:
  0.6 3.7 %pack.1 = (bf16[16,4,16,4096]{3,2,1,0:T(8,128)(2,1)S(1)}, bf16[2,256,512]{2,1,0:T(8,128)(2,1)S(1)}, bf16[128,4096]{1,0:T(8,128)(2,1)S(1)}) custom-call(bf16[2,16,16,4096]{3,2,1,0:T(8,128)(2,1)} %bitcast.5, bf16[2,16,16,4096]{3,2,1,0:T(8,128)(2,1)} %bitcast.6, bf16[1,256,512]{2,1,0:T(8,128)(2,1)} %wi_ref.1, bf16[1,256,512]{2,1,0:T(8,128)(2,1)} %wo_ref.1, ...), custom_call_target="tpu_custom_call" | custom-call | flops 8388608 | bytes 16777216 | tf_op jit(solution)/shard_map/pack/pallas_call | solution.py:78
  4.4 103.5 %all_to_all.15.a_ref.rows_ref = bf16[16,4,16,4096]{3,2,1,0:T(8,128)(2,1)S(1)} all-to-all(bf16[16,4,16,4096]{3,2,1,0:T(8,128)(2,1)S(1)} %get-tuple-element.50), channel_id=1, replica_groups=mesh['yh'=2,'x'=4,'c'=2,'z'=4,'yl'=2] {'yh','x','c'}, dimensions={0} | all-to-all | bytes 16777216 | tf_op jit(solution)/shard_map/all_to_all | solution.py:237
  107.9 4.1 %shard_map.76 = (bf16[8,2,2,16,2048]{4,3,2,1,0:T(8,128)(2,1)}, f32[512,128]{1,0:T(8,128)S(1)}, bf16[512,128]{1,0:T(8,128)(2,1)S(1)}) custom-call(bf16[16,4,16,4096]{3,2,1,0:T(8,128)(2,1)S(1)} %all_to_all.15.a_ref.rows_ref, bf16[128,4096]{1,0:T(8,128)(2,1)S(1)} %get-tuple-element.51.rxt_ref.far_rxt_ref), custom_call_target="tpu_custom_call" | custom-call | flops 3000000000 | bytes 12582912 | tf_op jit(solution)/shard_map/pallas_call | solution.py:238
  112.0 5.5 %all-to-all-start.1 = ((bf16[16,2,16,2048]{3,2,1,0:T(8,128)(2,1)}), bf16[16,2,16,2048]{3,2,1,0:T(8,128)(2,1)S(1)}, u32[]{:S(2)}, u32[]{:S(2)}) async-start(bf16[16,2,16,2048]{3,2,1,0:T(8,128)(2,1)} %bitcast.7), calls=%async_computation.1 | async-start | bytes 4194304 | tf_op jit(solution)/shard_map/all_to_all | solution.py:246
  117.6 0.8 collective-permute-start.5
  118.4 0.8 collective-permute-start.3
  119.2 0.7 collective-permute-start.1
  119.8 12.6 %collective-permute-done.5.refs_6_ = bf16[2,256,512]{2,1,0:T(8,128)(2,1)S(1)} collective-permute-done((bf16[2,256,512]{2,1,0:T(8,128)(2,1)S(1)}, bf16[2,256,512]{2,1,0:T(8,128)(2,1)S(1)}, u32[]{:S(2)}, u32[]{:S(2)}) %collective-permute-start.5) | collective-permute-done | bytes 524320 | tf_op jit(solution)/shard_map/ppermute | solution.py:228
  132.4 2.3 %collective-permute-done.3.refs_4_ = bf16[2,256,512]{2,1,0:T(8,128)(2,1)S(1)} collective-permute-done((bf16[2,256,512]{2,1,0:T(8,128)(2,1)S(1)}, bf16[2,256,512]{2,1,0:T(8,128)(2,1)S(1)}, u32[]{:S(2)}, u32[]{:S(2)}) %collective-permute-start.3) | collective-permute-done | bytes 524320 | tf_op jit(solution)/shard_map/ppermute | solution.py:228
  134.7 9.8 %collective-permute-done.1.refs_2_ = bf16[2,256,512]{2,1,0:T(8,128)(2,1)S(1)} collective-permute-done((bf16[2,256,512]{2,1,0:T(8,128)(2,1)S(1)}, bf16[2,256,512]{2,1,0:T(8,128)(2,1)S(1)}, u32[]{:S(2)}, u32[]{:S(2)}) %collective-permute-start.1) | collective-permute-done | bytes 524320 | tf_op jit(solution)/shard_map/ppermute | solution.py:228
  144.6 0.8 copy-done.5
  145.7 0.8 copy-done.8
  146.6 2.1 shard_map.78
  148.7 3.1 %collective-permute-start.8 = (bf16[256,512]{1,0:T(8,128)(2,1)S(1)}, bf16[256,512]{1,0:T(8,128)(2,1)S(1)}, u32[]{:S(2)}, u32[]{:S(2)}) collective-permute-start(bf16[256,512]{1,0:T(8,128)(2,1)S(1)} %get-tuple-element.59), channel_id=1, source_target_pairs={{0,64},{64,0},{1,65},{65,1},{2,66},{66,2},{3,67},{67,3},{4,68},{68... | collective-permute-start | bytes 786440 | tf_op jit(solution)/shard_map/ppermute | solution.py:232
  151.9 2.1 shard_map.77
  154.5 4.9 %collective-permute-done.8.other_ref = bf16[256,512]{1,0:T(8,128)(2,1)S(1)} collective-permute-done((bf16[256,512]{1,0:T(8,128)(2,1)S(1)}, bf16[256,512]{1,0:T(8,128)(2,1)S(1)}, u32[]{:S(2)}, u32[]{:S(2)}) %collective-permute-start.8) | collective-permute-done | bytes 262176 | tf_op jit(solution)/shard_map/ppermute | solution.py:232
  159.4 0.8 shard_map.79
  160.2 4.2 %collective-permute-done.7.other_ref = bf16[256,512]{1,0:T(8,128)(2,1)S(1)} collective-permute-done((bf16[256,512]{1,0:T(8,128)(2,1)S(1)}, bf16[256,512]{1,0:T(8,128)(2,1)S(1)}, u32[]{:S(2)}, u32[]{:S(2)}) %collective-permute-start.7) | collective-permute-done | bytes 262176 | tf_op jit(solution)/shard_map/ppermute | solution.py:232
  164.4 2.3 %shard_map.80 = (bf16[16,2,16,2048]{3,2,1,0:T(8,128)(2,1)}, bf16[256,512]{1,0:T(8,128)(2,1)S(1)}) custom-call(f32[256,512]{1,0:T(8,128)S(1)} %get-tuple-element.56.own_ref, bf16[256,512]{1,0:T(8,128)(2,1)S(1)} %collective-permute-done.7.other_ref, f32[256,512]{1,0:T(8,128)S(1)} %get-tuple-element.61.pre_ref, ...), custom_call_target="tpu_custom_call" | custom-call | flops 1000000000 | bytes 4194304 | tf_op jit(solution)/shard_map/pallas_call | solution.py:268
  166.7 6.9 %all-to-all-start.2 = ((bf16[16,2,16,2048]{3,2,1,0:T(8,128)(2,1)}), bf16[16,2,16,2048]{3,2,1,0:T(8,128)(2,1)}, u32[]{:S(2)}, u32[]{:S(2)}) async-start(bf16[16,2,16,2048]{3,2,1,0:T(8,128)(2,1)} %get-tuple-element.64), calls=%async_computation.2 | async-start | bytes 4194304 | tf_op jit(solution)/shard_map/all_to_all | solution.py:273
  173.7 1.3 shard_map.82
  176.1 0.9 collective-permute-done.9.got_ref
  179.4 1.4 collective-permute-start.16
  181.4 2.7 %collective-permute-start.18 = (bf16[256,512]{1,0:T(8,128)(2,1)S(1)}, bf16[256,512]{1,0:T(8,128)(2,1)S(1)}, u32[]{:S(2)}, u32[]{:S(2)}) collective-permute-start(bf16[256,512]{1,0:T(8,128)(2,1)S(1)} %get-tuple-element.96), channel_id=1, source_target_pairs={{0,48},{16,0},{32,16},{48,32},{1,49},{17,1},{33,17},{49,33},{2,50}... | collective-permute-start | bytes 786440 | tf_op jit(solution)/shard_map/ppermute | solution.py:228
  184.0 1.0 collective-permute-start.13
  185.0 5.2 %collective-permute-done.16.a_ref = bf16[256,512]{1,0:T(8,128)(2,1)S(1)} collective-permute-done((bf16[256,512]{1,0:T(8,128)(2,1)S(1)}, bf16[256,512]{1,0:T(8,128)(2,1)S(1)}, u32[]{:S(2)}, u32[]{:S(2)}) %collective-permute-start.16) | collective-permute-done | bytes 262176 | tf_op jit(solution)/shard_map/ppermute | solution.py:228
  190.2 1.1 collective-permute-start.15
  191.2 4.6 %collective-permute-done.17.b_ref = bf16[256,512]{1,0:T(8,128)(2,1)S(1)} collective-permute-done((bf16[256,512]{1,0:T(8,128)(2,1)S(1)}, bf16[256,512]{1,0:T(8,128)(2,1)S(1)}, u32[]{:S(2)}, u32[]{:S(2)}) %collective-permute-start.17) | collective-permute-done | bytes 262176 | tf_op jit(solution)/shard_map/ppermute | solution.py:228
  195.8 0.9 shard_map.88
  196.7 4.0 %all-to-all-done.2 = bf16[16,2,16,2048]{3,2,1,0:T(8,128)(2,1)} async-done(((bf16[16,2,16,2048]{3,2,1,0:T(8,128)(2,1)}), bf16[16,2,16,2048]{3,2,1,0:T(8,128)(2,1)}, u32[]{:S(2)}, u32[]{:S(2)}) %all-to-all-start.2) | async-done | bytes 2097184 | tf_op jit(solution)/shard_map/all_to_all | solution.py:273
  200.7 8.5 %shard_map.81 = bf16[32,16,4096]{2,1,0:T(8,128)(2,1)} custom-call(bf16[8,2,2,16,2048]{4,3,2,1,0:T(8,128)(2,1)} %bitcast.4.b_ref, f32[512,128]{1,0:T(8,128)S(1)} %get-tuple-element.65.probs_ref, bf16[512,128]{1,0:T(8,128)(2,1)S(1)} %get-tuple-element.54.mixing_ref, bf16[16,4,16,4096]{3,2,1,0:T(8,128)(2,1)} %copy-done, bf16[128,4096]{1,0:T(8,128)(2,1)} %copy-done.2), custom_call_target="tpu_custom_call" | custom-call | flops 4000000000 | bytes 16777216 | tf_op jit(solution)/shard_map/pallas_call | solution.py:291
  209.2 0.9 shard_map.87
  (43 shorter events, 5.0 us)
Async XLA Ops:
  4.3 103.6 %copy-start.2 = (bf16[128,4096]{1,0:T(8,128)(2,1)}, bf16[128,4096]{1,0:T(8,128)(2,1)S(1)}, u32[]{:S(2)}) copy-start(bf16[128,4096]{1,0:T(8,128)(2,1)S(1)} %get-tuple-element.51.rxt_ref.far_rxt_ref) | copy-start | bytes 3145732
  4.4 115.5 %copy-start.1 = (bf16[2,256,512]{2,1,0:T(8,128)(2,1)}, bf16[2,256,512]{2,1,0:T(8,128)(2,1)S(1)}, u32[]{:S(2)}) copy-start(bf16[2,256,512]{2,1,0:T(8,128)(2,1)S(1)} %get-tuple-element.55.refs_0_) | copy-start | bytes 1572868
  107.9 4.1 %copy-start = (bf16[16,4,16,4096]{3,2,1,0:T(8,128)(2,1)}, bf16[16,4,16,4096]{3,2,1,0:T(8,128)(2,1)S(1)}, u32[]{:S(2)}) copy-start(bf16[16,4,16,4096]{3,2,1,0:T(8,128)(2,1)S(1)} %all_to_all.15.a_ref.rows_ref) | copy-start | bytes 25165828
  112.0 34.6 %all-to-all-start.1 = ((bf16[16,2,16,2048]{3,2,1,0:T(8,128)(2,1)}), bf16[16,2,16,2048]{3,2,1,0:T(8,128)(2,1)S(1)}, u32[]{:S(2)}, u32[]{:S(2)}) async-start(bf16[16,2,16,2048]{3,2,1,0:T(8,128)(2,1)} %bitcast.7), calls=%async_computation.1 | async-start | bytes 4194304 | tf_op jit(solution)/shard_map/all_to_all | solution.py:246
  117.6 14.9 %collective-permute-start.5 = (bf16[2,256,512]{2,1,0:T(8,128)(2,1)S(1)}, bf16[2,256,512]{2,1,0:T(8,128)(2,1)S(1)}, u32[]{:S(2)}, u32[]{:S(2)}) collective-permute-start(bf16[2,256,512]{2,1,0:T(8,128)(2,1)S(1)} %get-tuple-element.55.refs_0_), channel_id=1, source_target_pairs={{0,48},{16,0},{32,16},{48,32},{1,49},{17,1},{33,17},{49,33},{2,50}... | collective-permute-start | bytes 1572872 | tf_op jit(solution)/shard_map/ppermute | solution.py:228
  118.4 16.3 %collective-permute-start.3 = (bf16[2,256,512]{2,1,0:T(8,128)(2,1)S(1)}, bf16[2,256,512]{2,1,0:T(8,128)(2,1)S(1)}, u32[]{:S(2)}, u32[]{:S(2)}) collective-permute-start(bf16[2,256,512]{2,1,0:T(8,128)(2,1)S(1)} %get-tuple-element.55.refs_0_), channel_id=1, source_target_pairs={{0,32},{16,48},{32,0},{48,16},{1,33},{17,49},{33,1},{49,17},{2,34}... | collective-permute-start | bytes 1572872 | tf_op jit(solution)/shard_map/ppermute | solution.py:228
  119.2 25.4 %collective-permute-start.1 = (bf16[2,256,512]{2,1,0:T(8,128)(2,1)S(1)}, bf16[2,256,512]{2,1,0:T(8,128)(2,1)S(1)}, u32[]{:S(2)}, u32[]{:S(2)}) collective-permute-start(bf16[2,256,512]{2,1,0:T(8,128)(2,1)S(1)} %get-tuple-element.55.refs_0_), channel_id=1, source_target_pairs={{0,16},{16,32},{32,48},{48,0},{1,17},{17,33},{33,49},{49,1},{2,18}... | collective-permute-start | bytes 1572872 | tf_op jit(solution)/shard_map/ppermute | solution.py:228
  119.8 24.8 %collective-permute-start = (bf16[2,256,512]{2,1,0:T(8,128)(2,1)S(1)}, bf16[2,256,512]{2,1,0:T(8,128)(2,1)S(1)}, u32[]{:S(2)}, u32[]{:S(2)}) collective-permute-start(bf16[2,256,512]{2,1,0:T(8,128)(2,1)S(1)} %get-tuple-element.55.refs_0_), channel_id=1, source_target_pairs={{0,8},{8,0},{1,9},{9,1},{2,10},{10,2},{3,11},{11,3},{4,12},{12,4},... | collective-permute-start | bytes 1572872 | tf_op jit(solution)/shard_map/ppermute | solution.py:232
  132.4 14.2 %copy-start.3 = (bf16[2,256,512]{2,1,0:T(8,128)(2,1)}, bf16[2,256,512]{2,1,0:T(8,128)(2,1)S(1)}, u32[]{:S(2)}) copy-start(bf16[2,256,512]{2,1,0:T(8,128)(2,1)S(1)} %collective-permute-done.5.refs_6_) | copy-start | bytes 1572868
  132.4 12.2 %collective-permute-start.6 = (bf16[2,256,512]{2,1,0:T(8,128)(2,1)S(1)}, bf16[2,256,512]{2,1,0:T(8,128)(2,1)S(1)}, u32[]{:S(2)}, u32[]{:S(2)}) collective-permute-start(bf16[2,256,512]{2,1,0:T(8,128)(2,1)S(1)} %collective-permute-done.5.refs_6_), channel_id=1, source_target_pairs={{0,8},{8,0},{1,9},{9,1},{2,10},{10,2},{3,11},{11,3},{4,12},{12,4},... | collective-permute-start | bytes 1572872 | tf_op jit(solution)/shard_map/ppermute | solution.py:232
  134.7 9.9 %copy-start.4 = (bf16[2,256,512]{2,1,0:T(8,128)(2,1)}, bf16[2,256,512]{2,1,0:T(8,128)(2,1)S(1)}, u32[]{:S(2)}) copy-start(bf16[2,256,512]{2,1,0:T(8,128)(2,1)S(1)} %collective-permute-done.3.refs_4_) | copy-start | bytes 1572868
  134.7 9.9 %collective-permute-start.4 = (bf16[2,256,512]{2,1,0:T(8,128)(2,1)S(1)}, bf16[2,256,512]{2,1,0:T(8,128)(2,1)S(1)}, u32[]{:S(2)}, u32[]{:S(2)}) collective-permute-start(bf16[2,256,512]{2,1,0:T(8,128)(2,1)S(1)} %collective-permute-done.3.refs_4_), channel_id=1, source_target_pairs={{0,8},{8,0},{1,9},{9,1},{2,10},{10,2},{3,11},{11,3},{4,12},{12,4},... | collective-permute-start | bytes 1572872 | tf_op jit(solution)/shard_map/ppermute | solution.py:232
  144.6 0.8 copy-start.5
  144.6 2.0 collective-permute-start.2
  144.6 0.9 copy-start.6
  144.6 1.1 copy-start.7
  145.7 0.8 copy-start.8
  148.7 10.7 %collective-permute-start.8 = (bf16[256,512]{1,0:T(8,128)(2,1)S(1)}, bf16[256,512]{1,0:T(8,128)(2,1)S(1)}, u32[]{:S(2)}, u32[]{:S(2)}) collective-permute-start(bf16[256,512]{1,0:T(8,128)(2,1)S(1)} %get-tuple-element.59), channel_id=1, source_target_pairs={{0,64},{64,0},{1,65},{65,1},{2,66},{66,2},{3,67},{67,3},{4,68},{68... | collective-permute-start | bytes 786440 | tf_op jit(solution)/shard_map/ppermute | solution.py:232
  153.9 10.5 %collective-permute-start.7 = (bf16[256,512]{1,0:T(8,128)(2,1)S(1)}, bf16[256,512]{1,0:T(8,128)(2,1)S(1)}, u32[]{:S(2)}, u32[]{:S(2)}) collective-permute-start(bf16[256,512]{1,0:T(8,128)(2,1)S(1)} %get-tuple-element.57), channel_id=1, source_target_pairs={{0,64},{64,0},{1,65},{65,1},{2,66},{66,2},{3,67},{67,3},{4,68},{68... | collective-permute-start | bytes 786440 | tf_op jit(solution)/shard_map/ppermute | solution.py:232
  166.7 34.0 %all-to-all-start.2 = ((bf16[16,2,16,2048]{3,2,1,0:T(8,128)(2,1)}), bf16[16,2,16,2048]{3,2,1,0:T(8,128)(2,1)}, u32[]{:S(2)}, u32[]{:S(2)}) async-start(bf16[16,2,16,2048]{3,2,1,0:T(8,128)(2,1)} %get-tuple-element.64), calls=%async_computation.2 | async-start | bytes 4194304 | tf_op jit(solution)/shard_map/all_to_all | solution.py:273
  175.0 2.0 collective-permute-start.9
  175.1 2.6 %collective-permute-start.10 = (bf16[2,256,512]{2,1,0:T(8,128)(2,1)S(1)}, bf16[2,256,512]{2,1,0:T(8,128)(2,1)S(1)}, u32[]{:S(2)}, u32[]{:S(2)}) collective-permute-start(bf16[2,256,512]{2,1,0:T(8,128)(2,1)S(1)} %get-tuple-element.72), channel_id=1, source_target_pairs={{0,8},{8,0},{1,9},{9,1},{2,10},{10,2},{3,11},{11,3},{4,12},{12,4},... | collective-permute-start | bytes 1572872 | tf_op jit(solution)/shard_map/ppermute | solution.py:232
  175.6 2.9 %collective-permute-start.11 = (bf16[2,256,512]{2,1,0:T(8,128)(2,1)S(1)}, bf16[2,256,512]{2,1,0:T(8,128)(2,1)S(1)}, u32[]{:S(2)}, u32[]{:S(2)}) collective-permute-start(bf16[2,256,512]{2,1,0:T(8,128)(2,1)S(1)} %get-tuple-element.75), channel_id=1, source_target_pairs={{0,8},{8,0},{1,9},{9,1},{2,10},{10,2},{3,11},{11,3},{4,12},{12,4},... | collective-permute-start | bytes 1572872 | tf_op jit(solution)/shard_map/ppermute | solution.py:232
  175.7 3.6 %collective-permute-start.12 = (bf16[2,256,512]{2,1,0:T(8,128)(2,1)S(1)}, bf16[2,256,512]{2,1,0:T(8,128)(2,1)S(1)}, u32[]{:S(2)}, u32[]{:S(2)}) collective-permute-start(bf16[2,256,512]{2,1,0:T(8,128)(2,1)S(1)} %get-tuple-element.78), channel_id=1, source_target_pairs={{0,8},{8,0},{1,9},{9,1},{2,10},{10,2},{3,11},{11,3},{4,12},{12,4},... | collective-permute-start | bytes 1572872 | tf_op jit(solution)/shard_map/ppermute | solution.py:232
  179.4 10.8 %collective-permute-start.16 = (bf16[256,512]{1,0:T(8,128)(2,1)S(1)}, bf16[256,512]{1,0:T(8,128)(2,1)S(1)}, u32[]{:S(2)}, u32[]{:S(2)}) collective-permute-start(bf16[256,512]{1,0:T(8,128)(2,1)S(1)} %get-tuple-element.94), channel_id=1, source_target_pairs={{0,32},{16,48},{32,0},{48,16},{1,33},{17,49},{33,1},{49,17},{2,34}... | collective-permute-start | bytes 786440 | tf_op jit(solution)/shard_map/ppermute | solution.py:228
  180.8 15.0 %collective-permute-start.17 = (bf16[256,512]{1,0:T(8,128)(2,1)S(1)}, bf16[256,512]{1,0:T(8,128)(2,1)S(1)}, u32[]{:S(2)}, u32[]{:S(2)}) collective-permute-start(bf16[256,512]{1,0:T(8,128)(2,1)S(1)} %get-tuple-element.95), channel_id=1, source_target_pairs={{0,16},{16,32},{32,48},{48,0},{1,17},{17,33},{33,49},{49,1},{2,18}... | collective-permute-start | bytes 786440 | tf_op jit(solution)/shard_map/ppermute | solution.py:228
  181.4 14.5 %collective-permute-start.18 = (bf16[256,512]{1,0:T(8,128)(2,1)S(1)}, bf16[256,512]{1,0:T(8,128)(2,1)S(1)}, u32[]{:S(2)}, u32[]{:S(2)}) collective-permute-start(bf16[256,512]{1,0:T(8,128)(2,1)S(1)} %get-tuple-element.96), channel_id=1, source_target_pairs={{0,48},{16,0},{32,16},{48,32},{1,49},{17,1},{33,17},{49,33},{2,50}... | collective-permute-start | bytes 786440 | tf_op jit(solution)/shard_map/ppermute | solution.py:228
  184.0 25.2 %collective-permute-start.13 = (bf16[256,512]{1,0:T(8,128)(2,1)S(1)}, bf16[256,512]{1,0:T(8,128)(2,1)S(1)}, u32[]{:S(2)}, u32[]{:S(2)}) collective-permute-start(bf16[256,512]{1,0:T(8,128)(2,1)S(1)} %get-tuple-element.80), channel_id=1, source_target_pairs={{0,32},{16,48},{32,0},{48,16},{1,33},{17,49},{33,1},{49,17},{2,34}... | collective-permute-start | bytes 786440 | tf_op jit(solution)/shard_map/ppermute | solution.py:228
  185.0 24.2 %collective-permute-start.14 = (bf16[256,512]{1,0:T(8,128)(2,1)S(1)}, bf16[256,512]{1,0:T(8,128)(2,1)S(1)}, u32[]{:S(2)}, u32[]{:S(2)}) collective-permute-start(bf16[256,512]{1,0:T(8,128)(2,1)S(1)} %get-tuple-element.81), channel_id=1, source_target_pairs={{0,16},{16,32},{32,48},{48,0},{1,17},{17,33},{33,49},{49,1},{2,18}... | collective-permute-start | bytes 786440 | tf_op jit(solution)/shard_map/ppermute | solution.py:228
  190.2 19.1 %collective-permute-start.15 = (bf16[256,512]{1,0:T(8,128)(2,1)S(1)}, bf16[256,512]{1,0:T(8,128)(2,1)S(1)}, u32[]{:S(2)}, u32[]{:S(2)}) collective-permute-start(bf16[256,512]{1,0:T(8,128)(2,1)S(1)} %get-tuple-element.82), channel_id=1, source_target_pairs={{0,48},{16,0},{32,16},{48,32},{1,49},{17,1},{33,17},{49,33},{2,50}... | collective-permute-start | bytes 786440 | tf_op jit(solution)/shard_map/ppermute | solution.py:228
